TPU v7x, 256 devices: a whole 4x4x8 slice. The times are simulated.
256 devices in a mesh: seq: 64 (over z, y, core), head: 4 (over x).
Axes of the slice: x: 4, y: 4, z: 8, core: 2. Of those that a mesh axis runs over, the one named last changes fastest.
Arguments:
- residual: bfloat16 [32768, 3072], P('seq', 'head'), may hold values from -6 to 6
- q_self: bfloat16 [32768, 3072], P('seq', 'head'), may hold values from -6 to 6
- k_self: bfloat16 [32768, 3072], P('seq', 'head'), may hold values from -6 to 6
- v_self: bfloat16 [32768, 3072], P('seq', 'head'), may hold values from -6 to 6
- w_out: bfloat16 [3072, 3072], P('head'), may hold values from -0.109375 to 0.109375
- norm_gain: float32 [3072], replicated, may hold values from 0.5 to 1.5
- w_query: bfloat16 [3072, 3072], P('seq', 'head')
- w_cache: bfloat16 [3072, 2048], P('seq', 'head')
- block_doc: int32 [64], replicated, may hold values from 0 to 15, never falling along the last dimension, each value on 1 to 5 neighbouring positions
- tail_len: int32 [64], replicated, may hold values from 1 to 512
Outputs:
- hidden: bfloat16 [32768, 3072], P('seq', 'head')
- cross_context: bfloat16 [32768, 3072], P('seq', 'head')
Inputs may be any that keep to these rules, and one draw needn't show every extreme that they name: block_doc never falls along the blocks; each document covers 1 to 5 consecutive blocks, and some document covers exactly 5. `tail_len`: read only for the last block of a document.
All inputs are finite; a program needn't handle non-finite values.
Results may differ from a plain program's by a relative error of at most 0.0078.
Values may be sent and summed in bfloat16 or wider, within the bound.
A program may use at most 128 MiB of HBM per device.

v0:
```python
import math

import jax
import jax.numpy as jnp
from jax import lax
from jax.sharding import PartitionSpec as P

D = 3072
HEAD_DIM = 128
WINDOW = 2048
DOC_MAX = 2560
WIN_BLOCKS = 4
DOC_BLOCKS = 5


EPSILON = 1e-06


def passed_along(block, axis, distance):
    devices = range(lax.axis_size(axis))
    route = [(i - distance, i) for i in devices if i - distance in devices]
    return lax.ppermute(block, axis, route)


def copy_for_each(x, axis):
    copies = jnp.broadcast_to(x, (lax.axis_size(axis), *x.shape))
    return lax.all_to_all(copies, axis, split_axis=0, concat_axis=0, tiled=True)


def taken_together(x, axis):
    everything = copy_for_each(x, axis)
    return jnp.sum(everything, axis=0)


def sent_together(arrays, axis, dim, along):
    widths = [a.shape[along] for a in arrays]
    both = jnp.concatenate(arrays, axis=along)
    result = lax.all_gather(both, axis, axis=dim, tiled=True)
    return tuple(jnp.split(result, [sum(widths[:k]) for k in range(1, len(widths))], axis=along))


def block_valid(block_doc, tail_len, tok_rows):
    following = jnp.concatenate([block_doc[1:], jnp.full((1,), -1, jnp.int32)])
    closing = following != block_doc
    within = jnp.arange(tok_rows, dtype=jnp.int32)
    return jnp.logical_or(jnp.logical_not(closing)[:, None], within[None, :] < tail_len[:, None])


def permitted(query_block, key_blocks, block_doc, valid_tokens, tok_rows, reach_tokens):
    inside = key_blocks >= 0
    safe_blocks = jnp.maximum(key_blocks, 0)
    own_doc = jnp.take(block_doc, query_block)
    same_doc = jnp.logical_and(inside, jnp.take(block_doc, safe_blocks) == own_doc)
    live_keys = jnp.logical_and(same_doc[:, None], jnp.take(valid_tokens, safe_blocks, axis=0))
    within = jnp.arange(tok_rows, dtype=jnp.int32)
    query_pos = query_block * tok_rows + within
    key_pos = (key_blocks[:, None] * tok_rows + within[None, :]).reshape(-1)
    distance = query_pos[:, None] - key_pos[None, :]
    near = jnp.logical_and(distance >= 0, distance < reach_tokens)
    return jnp.logical_and(near, live_keys.reshape(-1)[None, :])


def attend(queries, keys, values, allowed):
    row_count, head_count, head_dim = queries.shape
    group_size = head_count // keys.shape[1]
    scaling = 1.0 / math.sqrt(head_dim)

    def one_head(head_index):
        query_head = lax.dynamic_index_in_dim(queries, head_index, 1, keepdims=False)
        key_head = lax.dynamic_index_in_dim(keys, head_index // group_size, 1, keepdims=False)
        value_head = lax.dynamic_index_in_dim(values, head_index // group_size, 1, keepdims=False)
        scores = (
            lax.dot_general(
                query_head, key_head, (((1,), (1,)), ((), ())), preferred_element_type=jnp.float32
            )
            * scaling
        )
        scores = jnp.where(allowed, scores, -1e30)
        row_peak = jnp.max(scores, axis=1, keepdims=True)
        weights = jnp.exp(scores - row_peak)
        row_total = jnp.sum(weights, axis=1, keepdims=True)
        blended = jnp.dot(
            weights.astype(jnp.bfloat16), value_head, preferred_element_type=jnp.float32
        )
        return (blended / row_total).astype(jnp.bfloat16)

    per_head = lax.map(one_head, jnp.arange(head_count, dtype=jnp.int32))
    return jnp.transpose(per_head, (1, 0, 2)).reshape(row_count, head_count * head_dim)


def local(
    residual, q_self, k_self, v_self, w_out, norm_gain, w_query, w_cache, block_doc, tail_len
):
    tok_rows = residual.shape[0]
    local_heads = q_self.shape[1] // HEAD_DIM
    local_kv = w_cache.shape[1] // (2 * HEAD_DIM)
    query_width = local_heads * HEAD_DIM
    block_index = lax.axis_index("seq")
    valid_tokens = block_valid(block_doc, tail_len, tok_rows)
    stacked = jnp.concatenate([k_self, v_self], axis=1)
    earlier = []
    for offset in range(WIN_BLOCKS, 0, -1):
        earlier.append(passed_along(stacked, "seq", offset))
    window = jnp.concatenate(earlier + [stacked], axis=0)
    key_blocks = block_index - WIN_BLOCKS + jnp.arange(WIN_BLOCKS + 1, dtype=jnp.int32)
    allowed = permitted(block_index, key_blocks, block_doc, valid_tokens, tok_rows, WINDOW)
    context = attend(
        q_self.reshape(tok_rows, local_heads, HEAD_DIM),
        window[:, :query_width].reshape(-1, local_heads, HEAD_DIM),
        window[:, query_width:].reshape(-1, local_heads, HEAD_DIM),
        allowed,
    )
    partial_terms = jnp.dot(context, w_out, preferred_element_type=jnp.float32)
    own_columns = residual.shape[1]
    column_share = lax.psum_scatter(partial_terms, "head", scatter_dimension=1, tiled=True)
    hidden = (residual.astype(jnp.float32) + column_share).astype(jnp.bfloat16)
    wide = hidden.astype(jnp.float32)
    square_total = taken_together(jnp.sum(wide * wide, axis=1), "head")
    inverse_rms = lax.rsqrt(square_total / D + EPSILON)
    gain_share = lax.dynamic_slice_in_dim(
        norm_gain, lax.axis_index("head") * own_columns, own_columns, 0
    )
    normed_share = (wide * inverse_rms[:, None] * gain_share).astype(jnp.bfloat16)
    normed = lax.all_gather(normed_share, "head", axis=1, tiled=True)
    pieces = sent_together((w_query, w_cache), "seq", 0, 1)
    query_sum = jnp.dot(normed, pieces[0], preferred_element_type=jnp.float32)
    cache_sum = jnp.dot(normed, pieces[1], preferred_element_type=jnp.float32)
    cross_queries = query_sum.astype(jnp.bfloat16)
    cache_rows = cache_sum.astype(jnp.bfloat16)
    earlier_cache = []
    for offset in range(DOC_BLOCKS - 1, 0, -1):
        earlier_cache.append(passed_along(cache_rows, "seq", offset))
    history = jnp.concatenate(earlier_cache + [cache_rows], axis=0)
    doc_key_blocks = block_index - DOC_BLOCKS + 1 + jnp.arange(DOC_BLOCKS, dtype=jnp.int32)
    doc_allowed = permitted(block_index, doc_key_blocks, block_doc, valid_tokens, tok_rows, DOC_MAX)
    kv_width = local_kv * HEAD_DIM
    cross_context = attend(
        cross_queries.reshape(tok_rows, local_heads, HEAD_DIM),
        history[:, :kv_width].reshape(-1, local_kv, HEAD_DIM),
        history[:, kv_width:].reshape(-1, local_kv, HEAD_DIM),
        doc_allowed,
    )
    return (hidden, cross_context)


def solution(mesh):
    in_specs = (
        P("seq", "head"),
        P("seq", "head"),
        P("seq", "head"),
        P("seq", "head"),
        P("head", None),
        P(),
        P("seq", "head"),
        P("seq", "head"),
        P(),
        P(),
    )
    out_specs = (P("seq", "head"), P("seq", "head"))
    return jax.shard_map(local, mesh=mesh, in_specs=in_specs, out_specs=out_specs, check_vma=False)
```

profile of v0, /device:TPU:9, one launch (start us, length us, event | category | flops | bytes accessed | tf_op | source)
XLA Modules:
  0.0 448.2 jit_solution(11421778637095484967)
XLA Ops:
  11.0 5.1 %collective-permute-start = (bf16[512,1536]{0,1:T(8,128)(2,1)S(1)}, bf16[512,1536]{0,1:T(8,128)(2,1)}, u32[]{:S(2)}, u32[]{:S(2)}) collective-permute-start(bf16[512,1536]{0,1:T(8,128)(2,1)S(1)} %pad_maximum_fusion), channel_id=1, source_target_pairs={{0,16},{4,20},{8,24},{12,28},{16,32},{20,36},{24,40},{28,44},{32,4... | collective-permute-start | bytes 4718600 | tf_op jit(solution)/shard_map/ppermute | solution.py:22
  16.1 3.9 collective-permute-start.1
  20.0 3.2 collective-permute-start.2
  31.0 17.0 %collective-permute-done = bf16[512,1536]{0,1:T(8,128)(2,1)} collective-permute-done((bf16[512,1536]{0,1:T(8,128)(2,1)S(1)}, bf16[512,1536]{0,1:T(8,128)(2,1)}, u32[]{:S(2)}, u32[]{:S(2)}) %collective-permute-start) | collective-permute-done | bytes 1572896 | tf_op jit(solution)/shard_map/ppermute | solution.py:22
  49.5 36.1 %collective-permute-done.1 = bf16[512,1536]{0,1:T(8,128)(2,1)} collective-permute-done((bf16[512,1536]{0,1:T(8,128)(2,1)S(1)}, bf16[512,1536]{0,1:T(8,128)(2,1)}, u32[]{:S(2)}, u32[]{:S(2)}) %collective-permute-start.1) | collective-permute-done | bytes 1572896 | tf_op jit(solution)/shard_map/ppermute | solution.py:22
  87.1 30.2 %collective-permute-done.2 = bf16[512,1536]{0,1:T(8,128)(2,1)} collective-permute-done((bf16[512,1536]{0,1:T(8,128)(2,1)S(1)}, bf16[512,1536]{0,1:T(8,128)(2,1)}, u32[]{:S(2)}, u32[]{:S(2)}) %collective-permute-start.2) | collective-permute-done | bytes 1572896 | tf_op jit(solution)/shard_map/ppermute | solution.py:22
  118.9 15.4 %collective-permute-done.3 = bf16[512,1536]{0,1:T(8,128)(2,1)} collective-permute-done((bf16[512,1536]{0,1:T(8,128)(2,1)S(1)}, bf16[512,1536]{0,1:T(8,128)(2,1)}, u32[]{:S(2)}, u32[]{:S(2)}) %collective-permute-start.3) | collective-permute-done | bytes 1572896 | tf_op jit(solution)/shard_map/ppermute | solution.py:22
  135.9 3.4 fusion.70
  139.3 52.4 %while.27 = (s32[]{:T(128)}, bf16[6,512,128]{1,2,0:T(8,128)(2,1)S(1)}, s32[6]{0:T(128)S(1)}, bf16[512,6,128]{0,2,1:T(8,128)(2,1)}, bf16[2560,6,128]{0,2,1:T(8,12...) while((s32[]{:T(128)}, ...), condition=%wide.region_3.6_spmd.clone, body=%wide.region_0.5_spmd.clone.sunk | while | flops 686947328 | bytes 17852076 | solution.py:87
  141.9 3.2 fusion.88
  150.6 3.2 fusion.88
  159.3 3.2 fusion.88
  176.8 3.2 fusion.88
  191.7 7.0 %fusion.71 = f32[512,3072]{1,0:T(8,128)} fusion(bf16[512,768]{0,1:T(8,128)(2,1)S(1)} %bitcast.86, bf16[768,3072]{1,0:T(8,128)(2,1)} %param.22), kind=kOutput, calls=%fused_computation.92 | convolution fusion | flops 2415919104 | bytes 11796480 | tf_op jit(solution)/shard_map/dot_general | solution.py:113
  200.3 70.0 %reduce-scatter.2.cloned.1.call-done = f32[512,768]{1,0:T(8,128)} async-done(((f32[512,3072]{1,0:T(8,128)}), f32[512,768]{1,0:T(8,128)}) %reduce-scatter.2.cloned.1.call-update) | async-done | bytes 1572880 | tf_op jit(solution)/shard_map/reduce_scatter | solution.py:115
  272.7 3.2 all-to-all-start
  276.8 3.3 all-to-all-done
  281.3 7.1 %all-gather.5.cloned.1.call-done = bf16[3072,1280]{1,0:T(8,128)(2,1)} async-done(((bf16[48,1280]{1,0:T(8,128)(2,1)}), bf16[3072,1280]{1,0:T(8,128)(2,1)}) %all-gather.5.cloned.1.call-update) | async-done | bytes 7864336 | tf_op jit(solution)/shard_map/all_gather | solution.py:38
  288.4 41.4 %all-gather.3.cloned.1.call-done = bf16[512,3072]{1,0:T(8,128)(2,1)} async-done(((bf16[512,768]{1,0:T(8,128)(2,1)}), bf16[512,3072]{1,0:T(8,128)(2,1)}) %all-gather.3.cloned.1.call-update) | async-done | bytes 3145744 | tf_op jit(solution)/shard_map/all_gather | solution.py:124
  329.8 4.8 %fusion.62 = bf16[512,512]{1,0:T(8,128)(2,1)S(1)} fusion(bf16[512,3072]{1,0:T(8,128)(2,1)} %all-gather.3.cloned.1.call-done, bf16[3072,1280]{1,0:T(8,128)(2,1)} %all-gather.5.cloned.1.call-done), kind=kOutput, calls=%fused_computation.64 | convolution fusion | flops 1610874880 | bytes 6815744 | tf_op jit(solution)/shard_map/dot_general | solution.py:127
  334.6 4.7 %collective-permute-start.4 = (bf16[512,512]{1,0:T(8,128)(2,1)S(1)}, bf16[512,512]{1,0:T(8,128)(2,1)}, u32[]{:S(2)}, u32[]{:S(2)}) collective-permute-start(bf16[512,512]{1,0:T(8,128)(2,1)S(1)} %fusion.62), channel_id=1, source_target_pairs={{0,16},{4,20},{8,24},{12,28},{16,32},{20,36},{24,40},{28,44},{32,4... | collective-permute-start | bytes 1572872 | tf_op jit(solution)/shard_map/ppermute | solution.py:22
  339.3 4.3 collective-permute-start.5
  353.2 11.3 %collective-permute-done.5 = bf16[512,512]{1,0:T(8,128)(2,1)} collective-permute-done((bf16[512,512]{1,0:T(8,128)(2,1)S(1)}, bf16[512,512]{1,0:T(8,128)(2,1)}, u32[]{:S(2)}, u32[]{:S(2)}) %collective-permute-start.5) | collective-permute-done | bytes 524320 | tf_op jit(solution)/shard_map/ppermute | solution.py:22
  365.6 7.6 %collective-permute-done.6 = bf16[512,512]{1,0:T(8,128)(2,1)S(1)} collective-permute-done((bf16[512,512]{1,0:T(8,128)(2,1)S(1)}, bf16[512,512]{1,0:T(8,128)(2,1)S(1)}, u32[]{:S(2)}, u32[]{:S(2)}) %collective-permute-start.6) | collective-permute-done | bytes 524320 | tf_op jit(solution)/shard_map/ppermute | solution.py:22
  373.3 6.0 %collective-permute-done.7 = bf16[512,512]{1,0:T(8,128)(2,1)S(1)} collective-permute-done((bf16[512,512]{1,0:T(8,128)(2,1)S(1)}, bf16[512,512]{1,0:T(8,128)(2,1)S(1)}, u32[]{:S(2)}, u32[]{:S(2)}) %collective-permute-start.7) | collective-permute-done | bytes 524320 | tf_op jit(solution)/shard_map/ppermute | solution.py:22
  381.1 58.5 %while.28 = (s32[]{:T(128)}, bf16[6,512,128]{1,2,0:T(8,128)(2,1)S(1)}, s32[6]{0:T(128)S(1)}, bf16[512,6,128]{0,2,1:T(8,128)(2,1)S(1)}, bf16[2560,2,128]{2,0,1:T(...) while((s32[]{:T(128)}, ...), condition=%wide.region_10.13_spmd.clone, body=%wide.region_7.12_spmd.clone.sunk | while | flops 686947328 | bytes 17853756 | solution.py:87
  385.6 3.3 fusion.93
  395.4 3.3 fusion.93
  405.1 3.3 fusion.93
  414.9 3.3 fusion.93
  424.6 3.3 fusion.93
  434.4 3.3 fusion.93
  (134 shorter events, 78.7 us)
Async XLA Ops:
  8.0 17.8 %copy-start = (s32[64]{0:T(128)S(1)}, s32[64]{0:T(128)}, u32[]{:S(2)}) copy-start(s32[64]{0:T(128)} %param.26) | copy-start | bytes 772
  8.0 19.8 %copy-start.5 = (s32[64]{0:T(128)S(1)}, s32[64]{0:T(128)}, u32[]{:S(2)}) copy-start(s32[64]{0:T(128)} %param.27) | copy-start | bytes 772
  8.0 262.2 %reduce-scatter.2.cloned.1.call-start = ((), (), s32[]{:S(2)}) async-start(), calls=%async_computation.2 | async-start | bytes 7864320 | tf_op jit(solution)/shard_map/reduce_scatter | solution.py:115
  11.0 37.0 %collective-permute-start = (bf16[512,1536]{0,1:T(8,128)(2,1)S(1)}, bf16[512,1536]{0,1:T(8,128)(2,1)}, u32[]{:S(2)}, u32[]{:S(2)}) collective-permute-start(bf16[512,1536]{0,1:T(8,128)(2,1)S(1)} %pad_maximum_fusion), channel_id=1, source_target_pairs={{0,16},{4,20},{8,24},{12,28},{16,32},{20,36},{24,40},{28,44},{32,4... | collective-permute-start | bytes 4718600 | tf_op jit(solution)/shard_map/ppermute | solution.py:22
  16.1 69.5 %collective-permute-start.1 = (bf16[512,1536]{0,1:T(8,128)(2,1)S(1)}, bf16[512,1536]{0,1:T(8,128)(2,1)}, u32[]{:S(2)}, u32[]{:S(2)}) collective-permute-start(bf16[512,1536]{0,1:T(8,128)(2,1)S(1)} %pad_maximum_fusion), channel_id=1, source_target_pairs={{0,12},{4,16},{8,20},{12,24},{16,28},{20,32},{24,36},{28,40},{32,4... | collective-permute-start | bytes 4718600 | tf_op jit(solution)/shard_map/ppermute | solution.py:22
  20.0 97.4 %collective-permute-start.2 = (bf16[512,1536]{0,1:T(8,128)(2,1)S(1)}, bf16[512,1536]{0,1:T(8,128)(2,1)}, u32[]{:S(2)}, u32[]{:S(2)}) collective-permute-start(bf16[512,1536]{0,1:T(8,128)(2,1)S(1)} %pad_maximum_fusion), channel_id=1, source_target_pairs={{0,8},{4,12},{8,16},{12,20},{16,24},{20,28},{24,32},{28,36},{32,40... | collective-permute-start | bytes 4718600 | tf_op jit(solution)/shard_map/ppermute | solution.py:22
  23.2 111.1 %collective-permute-start.3 = (bf16[512,1536]{0,1:T(8,128)(2,1)S(1)}, bf16[512,1536]{0,1:T(8,128)(2,1)}, u32[]{:S(2)}, u32[]{:S(2)}) collective-permute-start(bf16[512,1536]{0,1:T(8,128)(2,1)S(1)} %pad_maximum_fusion), channel_id=1, source_target_pairs={{0,4},{4,8},{8,12},{12,16},{16,20},{20,24},{24,28},{28,32},{32,36}... | collective-permute-start | bytes 4718600 | tf_op jit(solution)/shard_map/ppermute | solution.py:22
  198.7 0.9 copy-start.3
  198.7 0.9 copy-start.4
  198.7 71.6 %copy-start.2 = (bf16[512,768]{1,0:T(8,128)(2,1)S(1)}, bf16[512,768]{1,0:T(8,128)(2,1)}, u32[]{:S(2)}) copy-start(bf16[512,768]{1,0:T(8,128)(2,1)} %param.18) | copy-start | bytes 2359300
  198.7 89.7 %all-gather.5.cloned.1.call-start = ((), (), s32[]{:S(2)}) async-start(), calls=%async_computation.4 | async-start | bytes 7987200 | tf_op jit(solution)/shard_map/all_gather | solution.py:38
  272.1 62.5 %copy-start.1 = (bf16[512,768]{1,0:T(8,128)(2,1)}, bf16[512,768]{1,0:T(8,128)(2,1)S(1)}, u32[]{:S(2)}) copy-start(bf16[512,768]{1,0:T(8,128)(2,1)S(1)} %get-tuple-element.341) | copy-start | bytes 2359300
  272.7 7.4 %all-to-all-start = ((f32[4,1,512]{2,1,0:T(1,128)}), f32[4,1,512]{2,1,0:T(1,128)S(1)}, u32[]{:S(2)}, u32[]{:S(2)}) async-start(f32[4,1,512]{2,1,0:T(1,128)} %broadcast_in_dim.64), calls=%async_computation.1 | async-start | bytes 16384 | tf_op jit(solution)/shard_map/all_to_all | solution.py:27
  276.0 53.8 %all-gather.3.cloned.1.call-start = ((), (), s32[]{:S(2)}) async-start(), calls=%async_computation.3 | async-start | bytes 3932160 | tf_op jit(solution)/shard_map/all_gather | solution.py:124
  329.8 19.4 %copy-start.6 = (bf16[3072,1280]{1,0:T(8,128)(2,1)S(1)}, bf16[3072,1280]{1,0:T(8,128)(2,1)}, u32[]{:S(2)}) copy-start(bf16[3072,1280]{1,0:T(8,128)(2,1)} %all-gather.5.cloned.1.call-done) | copy-start | bytes 23592964
  329.8 19.4 %copy-start.7 = (bf16[512,3072]{1,0:T(8,128)(2,1)S(1)}, bf16[512,3072]{1,0:T(8,128)(2,1)}, u32[]{:S(2)}) copy-start(bf16[512,3072]{1,0:T(8,128)(2,1)} %all-gather.3.cloned.1.call-done) | copy-start | bytes 9437188
  334.6 17.5 %collective-permute-start.4 = (bf16[512,512]{1,0:T(8,128)(2,1)S(1)}, bf16[512,512]{1,0:T(8,128)(2,1)}, u32[]{:S(2)}, u32[]{:S(2)}) collective-permute-start(bf16[512,512]{1,0:T(8,128)(2,1)S(1)} %fusion.62), channel_id=1, source_target_pairs={{0,16},{4,20},{8,24},{12,28},{16,32},{20,36},{24,40},{28,44},{32,4... | collective-permute-start | bytes 1572872 | tf_op jit(solution)/shard_map/ppermute | solution.py:22
  339.3 25.3 %collective-permute-start.5 = (bf16[512,512]{1,0:T(8,128)(2,1)S(1)}, bf16[512,512]{1,0:T(8,128)(2,1)}, u32[]{:S(2)}, u32[]{:S(2)}) collective-permute-start(bf16[512,512]{1,0:T(8,128)(2,1)S(1)} %fusion.62), channel_id=1, source_target_pairs={{0,12},{4,16},{8,20},{12,24},{16,28},{20,32},{24,36},{28,40},{32,4... | collective-permute-start | bytes 1572872 | tf_op jit(solution)/shard_map/ppermute | solution.py:22
  343.6 29.7 %collective-permute-start.6 = (bf16[512,512]{1,0:T(8,128)(2,1)S(1)}, bf16[512,512]{1,0:T(8,128)(2,1)S(1)}, u32[]{:S(2)}, u32[]{:S(2)}) collective-permute-start(bf16[512,512]{1,0:T(8,128)(2,1)S(1)} %fusion.62), channel_id=1, source_target_pairs={{0,8},{4,12},{8,16},{12,20},{16,24},{20,28},{24,32},{28,36},{32,40... | collective-permute-start | bytes 1572872 | tf_op jit(solution)/shard_map/ppermute | solution.py:22
  346.7 32.5 %collective-permute-start.7 = (bf16[512,512]{1,0:T(8,128)(2,1)S(1)}, bf16[512,512]{1,0:T(8,128)(2,1)S(1)}, u32[]{:S(2)}, u32[]{:S(2)}) collective-permute-start(bf16[512,512]{1,0:T(8,128)(2,1)S(1)} %fusion.62), channel_id=1, source_target_pairs={{0,4},{4,8},{8,12},{12,16},{16,20},{20,24},{24,28},{28,32},{32,36}... | collective-permute-start | bytes 1572872 | tf_op jit(solution)/shard_map/ppermute | solution.py:22
Sparse Core Ops, SparseCore 0:
  198.8 71.3 reduce-scatter.1
Sparse Core Ops, SparseCore 1:
  201.9 86.4 all-gather.4
  290.6 39.1 all-gather.2
where the time goes:
time: 452 us; the launch traced here: 448 us
  waiting for transfers between devices  246 us (54%)
  matrix products  71 us (16%)
  loops' own time  35.3 us (8%)
  local copies, waits for them, and re-layouts  33 us (7%)
  starting transfers between devices  32.7 us (7%)
  between operations  16.4 us (4%)
  other arithmetic  14.4 us (3%)
    ppermute x8, waiting for transfers between devices, passed_along(): return lax.ppermute(block, axis, route)  124 us
    reduce_scatter x1, waiting for transfers between devices, local(): lax.psum_scatter(partial_terms, 'head', scatter_dimension=1, tiled=True)  70 us
    all_gather x1, waiting for transfers between devices, local(): normed = lax.all_gather(normed_share, 'head', axis=1, tiled=True)  41.4 us
    dot_general x12, matrix products, one_head(): lax.dot_general(query_head, key_head, (((1,), (1,)), ((), ())), preferred...  39.3 us
    another operation x2, loops' own time, attend(): per_head = lax.map(one_head, jnp.arange(head_count, dtype=jnp.int32))  35.3 us
    ppermute x8, starting transfers between devices, passed_along(): return lax.ppermute(block, axis, route)  29.3 us
    dot_general x12, matrix products, one_head(): jnp.dot(weights.astype(jnp.bfloat16), value_head, preferred_element_type=...  17.4 us
    unnamed x29, local copies, waits for them, and re-layouts  15.8 us
  transfers between devices with their start and end apart: 12, of which 11 were waited for; matrix products, arithmetic and copies ran while one was open for 4% of the time, Pallas kernels for 0%

commit v1 on v0

v1 whole, which is shorter than its diff:
```python
import functools
import math

import jax
import jax.numpy as jnp
from jax import lax
from jax.experimental import pallas as pl
from jax.experimental.pallas import tpu as pltpu
from jax.sharding import PartitionSpec as P

D = 3072
HEAD_DIM = 128
ROWS = 512
NBLK = 64
HEADS = 6
SLOTS = 5
WIDTH = HEADS * HEAD_DIM
HALF = WIDTH // 2
EPSILON = 1e-06
SCALE = 1.0 / math.sqrt(HEAD_DIM)
MASKED = -1e30
TILE = 128

MESH = pl.DeviceIdType.MESH
F32 = jnp.float32
BF16 = jnp.bfloat16

PLUS = (0, 3)
MINUS = (1, 2, 4, 5)


class Copies:
    def __init__(self, send_sem, recv_sem):
        self.send_sem, self.recv_sem = send_sem, recv_sem
        self.made = {}

    def make(self, name, src, dst, device):
        if name not in self.made:
            self.made[name] = len(self.made)
        n = self.made[name]
        return pltpu.make_async_remote_copy(
            src_ref=src,
            dst_ref=dst,
            send_sem=self.send_sem.at[n],
            recv_sem=self.recv_sem.at[n],
            device_id=device,
            device_id_type=MESH,
        )


class Place:
    def __init__(self):
        i = lax.axis_index("seq")
        x = lax.axis_index("head")
        self.i, self.x = i, x
        c = i % 2
        y = (i // 2) % 4
        z = i // 8
        self.c, self.y, self.z = c, y, z

        def at(zz, yy, cc):
            return ((zz + 8) % 8 * 4 + yy) * 2 + cc

        up = (y + 1) % 4
        down = (y + 3) % 4
        self.next_chip = (at(z + (y + 1) // 4, up, c), x)
        self.prev_chip = (at(z - (6 - y) // 6, down, c), x)
        self.relay_to = (at(z, down, c), x)
        self.relay_from = (at(z, up, c), x)
        self.pass_to = (at(z + (up + 2) // 4, down, c), x)
        self.pass_from = (at(z - ((y + 2) % 4) // 2, up, c), x)
        self.partner = (i + 1 - 2 * c, x)
        self.right = (i, (x + 1) % 4)
        self.left = (i, (x + 3) % 4)


def greet(devices):
    barrier = pltpu.get_barrier_semaphore()
    for device in devices:
        pl.semaphore_signal(barrier, inc=1, device_id=device, device_id_type=MESH)
    pl.semaphore_wait(barrier, len(devices))


def key_limits(doc_ref, tail_ref, i):
    limits = []
    own = doc_ref[i]
    for d in range(SLOTS):
        j = jnp.maximum(i - d, 0)
        doc = doc_ref[j]
        after = doc_ref[jnp.minimum(j + 1, NBLK - 1)]
        closing = jnp.logical_or(j == NBLK - 1, after != doc)
        count = jnp.where(closing, tail_ref[j], ROWS)
        seen = jnp.logical_and(i - d >= 0, doc == own)
        limits.append(jnp.where(seen, count, 0))
    return limits


def attend_tile(q, keys, values, limits, row0, windowed):
    rows = q.shape[0]
    query_at = row0 + lax.broadcasted_iota(jnp.int32, (rows, ROWS), 0)
    key_at = lax.broadcasted_iota(jnp.int32, (rows, ROWS), 1)
    lane = lax.broadcasted_iota(jnp.int32, (1, ROWS), 1)
    scores = []
    for d in range(SLOTS):
        s = lax.dot_general(q, keys(d), (((1,), (1,)), ((), ())), preferred_element_type=F32)
        s = s * SCALE + jnp.where(lane < limits[d], 0.0, MASKED)
        if d == 0:
            s = jnp.where(key_at <= query_at, s, MASKED)
        if d == SLOTS - 1 and windowed:
            s = jnp.where(key_at > query_at, s, MASKED)
        scores.append(s)
    peak = functools.reduce(jnp.maximum, scores)
    peak = jnp.max(peak, axis=1, keepdims=True)
    total = None
    blended = None
    for d in range(SLOTS):
        weights = jnp.exp(scores[d] - peak)
        total = weights if total is None else total + weights
        part = jnp.dot(weights.astype(BF16), values(d), preferred_element_type=F32)
        blended = part if blended is None else blended + part
    return (blended / jnp.sum(total, axis=1, keepdims=True)).astype(BF16)


def self_kernel(
    doc_ref, tail_ref, q_ref, res_ref, k_hbm, v_hbm, wo_hbm, hidden_ref,
    kv, relay, ctx, woc, wrelay, acc, local_sem, send_sem, recv_sem,
):
    here = Place()
    i, x, c = here.i, here.x, here.c
    copies = Copies(send_sem, recv_sem)
    started = []
    right_x, left_x, far_x = (x + 1) % 4, (x + 3) % 4, (x + 2) % 4

    local = []
    for h in range(HEADS):
        cols = pl.ds(h * HEAD_DIM, HEAD_DIM)
        one = pltpu.make_async_copy(k_hbm.at[:, cols], kv.at[SLOTS - 1, h, 0], local_sem.at[2 * h])
        two = pltpu.make_async_copy(v_hbm.at[:, cols], kv.at[SLOTS - 1, h, 1], local_sem.at[2 * h + 1])
        one.start()
        two.start()
        local.append((one, two))
    own_rows = pl.ds(pl.multiple_of(x * WIDTH, WIDTH), WIDTH)
    own_cols = pl.ds(pl.multiple_of(x * WIDTH, WIDTH), WIDTH)
    own_w = pltpu.make_async_copy(wo_hbm.at[:, own_cols], woc.at[own_rows], local_sem.at[2 * HEADS])
    own_w.start()

    greet([
        here.next_chip, here.prev_chip, here.relay_to, here.relay_from, here.pass_to, here.pass_from,
        here.partner, here.right, here.left,
    ])

    def go(copy):
        copy.start()
        started.append(copy)

    def forth(h):
        return copies.make(("forth", h), kv.at[4, h], kv.at[1, h], here.next_chip)

    def again(h):
        return copies.make(("again", h), kv.at[1, h], kv.at[3, h], here.next_chip)

    def back(h):
        return copies.make(("back", h), kv.at[4, h], relay.at[MINUS.index(h)], here.relay_to)

    def over(h):
        return copies.make(("over", h), relay.at[MINUS.index(h)], kv.at[3, h], here.pass_to)

    def twin_near(h):
        return copies.make(("near", h), kv.at[1, h], kv.at[2 * (1 - c), h], here.partner)

    def twin_far(h):
        return copies.make(("far", h), kv.at[4 - c, h], kv.at[2 * c, h], here.partner)

    def w_rows(block, first, count):
        return pl.ds(pl.multiple_of(block * WIDTH + c * HALF + first, 64), count)

    def w_cols(block):
        return pl.ds(pl.multiple_of(block * WIDTH, WIDTH), WIDTH)

    quarter = HALF // 2
    c_half = pl.ds(pl.multiple_of(c * HALF, HALF), HALF)
    c_one = pl.ds(pl.multiple_of(c * HALF, 64), quarter)
    c_two = pl.ds(pl.multiple_of(c * HALF + quarter, 64), quarter)
    w_right = copies.make("wr", wo_hbm.at[c_half, w_cols(right_x)], woc.at[w_rows(x, 0, HALF)], here.right)
    w_left = copies.make("wl", wo_hbm.at[c_half, w_cols(left_x)], woc.at[w_rows(x, 0, HALF)], here.left)
    w_far_r = copies.make("wfr", wo_hbm.at[c_one, w_cols(far_x)], wrelay.at[0], here.right)
    w_far_l = copies.make("wfl", wo_hbm.at[c_two, w_cols(far_x)], wrelay.at[1], here.left)
    w_on_r = copies.make("wor", wrelay.at[0], woc.at[w_rows(left_x, 0, quarter)], here.right)
    w_on_l = copies.make("wol", wrelay.at[1], woc.at[w_rows(right_x, quarter, quarter)], here.left)

    def w_twin(name, block):
        rows = w_rows(block, 0, HALF)
        return copies.make(("wt", name), woc.at[rows], woc.at[rows], here.partner)

    w_twin_l = w_twin("l", left_x)
    w_twin_r = w_twin("r", right_x)
    w_twin_f = w_twin("f", far_x)

    def ctx_cols(block, h):
        return pl.ds(pl.multiple_of(block * WIDTH + h * HEAD_DIM, HEAD_DIM), HEAD_DIM)

    upper, lower = pl.ds(0, ROWS // 2), pl.ds(ROWS // 2, ROWS // 2)

    def ctx_right(h):
        return copies.make(("cr", h), ctx.at[:, ctx_cols(x, h)], ctx.at[:, ctx_cols(x, h)], here.right)

    def ctx_left(h):
        return copies.make(("cl", h), ctx.at[:, ctx_cols(x, h)], ctx.at[:, ctx_cols(x, h)], here.left)

    def ctx_on_right(h):
        part = ctx.at[upper, ctx_cols(left_x, h)]
        return copies.make(("cor", h), part, part, here.right)

    def ctx_on_left(h):
        part = ctx.at[lower, ctx_cols(right_x, h)]
        return copies.make(("col", h), part, part, here.left)

    limits = key_limits(doc_ref, tail_ref, i)

    def attend(h):
        def slot(d):
            return (d + SLOTS - 1) % SLOTS

        def tile(t, carry):
            row0 = pl.multiple_of(t * TILE, TILE)
            rows = pl.ds(row0, TILE)
            q = q_ref[rows, h * HEAD_DIM:(h + 1) * HEAD_DIM]
            out = attend_tile(
                q, lambda d: kv[slot(d), h, 0], lambda d: kv[slot(d), h, 1], limits, row0, True
            )
            ctx[rows, ctx_cols(x, h)] = out
            return carry

        lax.fori_loop(0, ROWS // TILE, tile, 0)
        go(ctx_right(h))
        go(ctx_left(h))

    def pass_context(h):
        ctx_right(h).wait_recv()
        go(ctx_on_right(h))
        ctx_left(h).wait_recv()
        go(ctx_on_left(h))

    for h in (0, 1, 2):
        for copy in local[h]:
            copy.wait()
    go(forth(0))
    go(back(1))
    go(w_right)
    go(w_left)
    go(w_far_r)
    go(w_far_l)
    go(forth(1))
    go(back(2))
    for h in (3, 4, 5):
        for copy in local[h]:
            copy.wait()
    own_w.wait()

    forth(0).wait_recv()
    go(again(0))
    go(forth(3))
    go(twin_near(0))
    back(1).wait_recv()
    go(over(1))
    go(back(4))
    forth(1).wait_recv()
    go(forth(2))
    go(twin_near(1))
    back(2).wait_recv()
    go(over(2))
    go(back(5))
    again(0).wait_recv()
    go(twin_far(0))
    over(1).wait_recv()
    go(twin_far(1))
    twin_near(0).wait_recv()
    twin_far(0).wait_recv()
    attend(0)
    w_right.wait_recv()
    go(w_twin_l)
    w_left.wait_recv()
    go(w_twin_r)
    w_far_r.wait_recv()
    go(w_on_r)
    w_far_l.wait_recv()
    go(w_on_l)
    twin_near(1).wait_recv()
    twin_far(1).wait_recv()
    attend(1)
    forth(3).wait_recv()
    go(again(3))
    go(forth(4))
    go(forth(5))
    go(twin_near(3))
    back(4).wait_recv()
    go(over(4))
    forth(2).wait_recv()
    go(twin_near(2))
    over(2).wait_recv()
    go(twin_far(2))
    w_on_r.wait_recv()
    w_on_l.wait_recv()
    go(w_twin_f)
    twin_near(2).wait_recv()
    twin_far(2).wait_recv()
    attend(2)
    pass_context(0)
    pass_context(1)
    back(5).wait_recv()
    go(over(5))
    again(3).wait_recv()
    go(twin_far(3))
    twin_near(3).wait_recv()
    twin_far(3).wait_recv()
    attend(3)
    pass_context(2)
    forth(4).wait_recv()
    go(twin_near(4))
    over(4).wait_recv()
    go(twin_far(4))
    twin_near(4).wait_recv()
    twin_far(4).wait_recv()
    attend(4)
    pass_context(3)
    forth(5).wait_recv()
    go(twin_near(5))
    over(5).wait_recv()
    go(twin_far(5))
    twin_near(5).wait_recv()
    twin_far(5).wait_recv()
    attend(5)
    pass_context(4)
    for copy in (w_twin_l, w_twin_r, w_twin_f):
        copy.wait_recv()
    for h in range(4):
        ctx_on_right(h).wait_recv()
        ctx_on_left(h).wait_recv()

    def project(first, count, seed, store):
        def tile(t, carry):
            rows = pl.ds(pl.multiple_of(t * TILE, TILE), TILE)
            total = seed(rows)
            for block in range(4):
                at = block * WIDTH + first
                total = total + jnp.dot(
                    ctx[rows, at:at + count], woc[at:at + count, :], preferred_element_type=F32
                )
            store(rows, total)
            return carry

        lax.fori_loop(0, ROWS // TILE, tile, 0)

    def keep(rows, total):
        acc[rows, :] = total

    def finish(rows, total):
        hidden_ref[rows, :] = (res_ref[rows, :].astype(F32) + total).astype(BF16)

    project(0, 4 * HEAD_DIM, lambda rows: jnp.zeros((TILE, WIDTH), F32), keep)
    pass_context(5)
    for h in (4, 5):
        ctx_on_right(h).wait_recv()
        ctx_on_left(h).wait_recv()
    project(4 * HEAD_DIM, 2 * HEAD_DIM, lambda rows: acc[rows, :], finish)
    for copy in started:
        copy.wait_send()


N_SELF = 62


def self_layer(doc, tail, q, res, k, v, wo):
    any_spec = pl.BlockSpec(memory_space=pl.ANY)
    vmem = pl.BlockSpec(memory_space=pltpu.VMEM)
    smem = pl.BlockSpec(memory_space=pltpu.SMEM)
    return pl.pallas_call(
        self_kernel,
        out_shape=jax.ShapeDtypeStruct((ROWS, WIDTH), BF16),
        in_specs=[smem, smem, vmem, vmem, any_spec, any_spec, any_spec],
        out_specs=vmem,
        scratch_shapes=[
            pltpu.VMEM((SLOTS, HEADS, 2, ROWS, HEAD_DIM), BF16),
            pltpu.VMEM((len(MINUS), 2, ROWS, HEAD_DIM), BF16),
            pltpu.VMEM((ROWS, D), BF16),
            pltpu.VMEM((D, WIDTH), BF16),
            pltpu.VMEM((2, HALF // 2, WIDTH), BF16),
            pltpu.VMEM((ROWS, WIDTH), F32),
            pltpu.SemaphoreType.DMA((2 * HEADS + 1,)),
            pltpu.SemaphoreType.DMA((N_SELF,)),
            pltpu.SemaphoreType.DMA((N_SELF,)),
        ],
        compiler_params=pltpu.CompilerParams(
            collective_id=0, has_side_effects=True, vmem_limit_bytes=56 * 1024 * 1024
        ),
        cost_estimate=pl.CostEstimate(
            flops=60_000_000_000, bytes_accessed=20_000_000, transcendentals=0
        ),
        name="self_layer",
    )(doc, tail, q, res, k, v, wo)


def cross_kernel(doc_ref, tail_ref, q_ref, hist_ref, out_ref):
    i = lax.axis_index("seq")
    limits = key_limits(doc_ref, tail_ref, i)

    def slot_rows(d):
        at = (SLOTS - 1 - d) * ROWS
        return slice(at, at + ROWS)

    for h in range(HEADS):
        g = h // 3

        def tile(t, carry):
            row0 = pl.multiple_of(t * TILE, TILE)
            rows = pl.ds(row0, TILE)
            q = q_ref[rows, h * HEAD_DIM:(h + 1) * HEAD_DIM]
            out_ref[rows, h * HEAD_DIM:(h + 1) * HEAD_DIM] = attend_tile(
                q,
                lambda d: hist_ref[slot_rows(d), g * HEAD_DIM:(g + 1) * HEAD_DIM],
                lambda d: hist_ref[slot_rows(d), (2 + g) * HEAD_DIM:(3 + g) * HEAD_DIM],
                limits, row0, False,
            )
            return carry

        lax.fori_loop(0, ROWS // TILE, tile, 0)


def cross_attend(doc, tail, q, hist):
    vmem = pl.BlockSpec(memory_space=pltpu.VMEM)
    smem = pl.BlockSpec(memory_space=pltpu.SMEM)
    return pl.pallas_call(
        cross_kernel,
        out_shape=jax.ShapeDtypeStruct((ROWS, WIDTH), BF16),
        in_specs=[smem, smem, vmem, vmem],
        out_specs=vmem,
        compiler_params=pltpu.CompilerParams(vmem_limit_bytes=48 * 1024 * 1024),
        cost_estimate=pl.CostEstimate(
            flops=12_000_000_000, bytes_accessed=5_000_000, transcendentals=0
        ),
        name="cross_attend",
    )(doc, tail, q, hist)


def passed_along(block, axis, distance):
    devices = range(lax.axis_size(axis))
    route = [(i - distance, i) for i in devices if i - distance in devices]
    return lax.ppermute(block, axis, route)


def local(
    residual, q_self, k_self, v_self, w_out, norm_gain, w_query, w_cache, block_doc, tail_len
):
    weights = lax.all_gather(
        jnp.concatenate([w_query, w_cache], axis=1), "seq", axis=0, tiled=True
    )
    hidden = self_layer(block_doc, tail_len, q_self, residual, k_self, v_self, w_out)
    everything = lax.all_gather(hidden, "head", axis=1, tiled=True)
    wide = everything.astype(F32)
    mean_square = jnp.mean(wide * wide, axis=1, keepdims=True)
    normed = (wide * lax.rsqrt(mean_square + EPSILON) * norm_gain).astype(BF16)
    cache_rows = jnp.dot(normed, weights[:, WIDTH:], preferred_element_type=F32).astype(BF16)
    cross_queries = jnp.dot(normed, weights[:, :WIDTH], preferred_element_type=F32).astype(BF16)
    earlier = [passed_along(cache_rows, "seq", offset) for offset in range(SLOTS - 1, 0, -1)]
    history = jnp.concatenate(earlier + [cache_rows], axis=0)
    return (hidden, cross_attend(block_doc, tail_len, cross_queries, history))


def solution(mesh):
    in_specs = (
        P("seq", "head"),
        P("seq", "head"),
        P("seq", "head"),
        P("seq", "head"),
        P("head", None),
        P(),
        P("seq", "head"),
        P("seq", "head"),
        P(),
        P(),
    )
    out_specs = (P("seq", "head"), P("seq", "head"))
    return jax.shard_map(local, mesh=mesh, in_specs=in_specs, out_specs=out_specs, check_vma=False)
```

time: 452 us -> 309 us (0.68)
  the two profiles are of different devices: /device:TPU:9 before, /device:TPU:41 now
where the time goes in v1:
time: 309 us
  waiting for transfers between devices  172 us (56%)
  Pallas kernels  99.2 us (32%)
  between operations  14.2 us (5%)
  starting transfers between devices  12.6 us (4%)
  matrix products  6.6 us (2%)
  other arithmetic  3.39 us (1%)
    all_gather x1, waiting for transfers between devices, local(): lax.all_gather(jnp.concatenate([w_query, w_cache], axis=1), 'seq', axis=0...  82 us
    pallas_call x1, Pallas kernels, self_layer(): pl.pallas_call(self_kernel, out_shape=jax.ShapeDtypeStruct((ROWS, WIDTH),...  77.5 us
    ppermute x4, waiting for transfers between devices, passed_along(): return lax.ppermute(block, axis, route)  48 us
    all_gather x1, waiting for transfers between devices, local(): everything = lax.all_gather(hidden, 'head', axis=1, tiled=True)  41.4 us
    pallas_call x1, Pallas kernels, cross_attend(): pl.pallas_call(cross_kernel, out_shape=jax.ShapeDtypeStruct((ROWS, WIDTH)...  21.7 us
    ppermute x4, starting transfers between devices, passed_along(): return lax.ppermute(block, axis, route)  12.5 us
  transfers between devices with their start and end apart: 6, of which 3 were waited for; matrix products, arithmetic and copies ran while one was open for 2% of the time, Pallas kernels for 0%

profile of v1, /device:TPU:41, one launch (start us, length us, event | category | flops | bytes accessed | tf_op | source)
XLA Modules:
  0.0 308.7 jit_solution(12091997815534052548)
XLA Ops:
  7.2 0.0 copy-start.5
  7.2 0.0 copy-start.4
  7.2 0.0 all-gather.3.cloned.1.call-start
  7.2 77.5 %self_layer.1 = bf16[512,768]{1,0:T(8,128)(2,1)} custom-call(s32[64]{0:T(128)} %doc_ref.3, s32[64]{0:T(128)} %tail_ref.3, bf16[512,768]{1,0:T(8,128)(2,1)} %q_ref.1, bf16[512,768]{1,0:T(8,128)(2,1)} %res_ref.1, bf16[512,768]{1,0:T(8,128)(2,1)} %k_hbm.1, bf16[512,768]{1,0:T(8,128)(2,1)} %v_hbm.1, bf16[768,3072]{1,0:T(8,128)(2,1)} %wo_hbm.1), custom_call_target="tpu_custom_call" | custom-call | flops 60000002048 | bytes 20000000 | tf_op jit(solution)/shard_map/self_layer/pallas_call | solution.py:377
  84.7 0.0 copy-start.7
  84.8 0.0 all-gather.3.cloned.1.call-update
  84.8 0.0 all-gather.5.cloned.1.call-start
  84.8 0.0 copy-done.5
  84.9 0.7 pad_maximum_fusion
  85.5 0.0 all-gather.5.cloned.1.call-update
  85.5 41.4 %all-gather.3.cloned.1.call-done = bf16[512,3072]{1,0:T(8,128)(2,1)} async-done(((bf16[512,768]{1,0:T(8,128)(2,1)}), bf16[512,3072]{1,0:T(8,128)(2,1)}) %all-gather.3.cloned.1.call-update) | async-done | bytes 3145744 | tf_op jit(solution)/shard_map/all_gather | solution.py:458
  127.0 2.7 fusion
  129.7 82.0 %all-gather.5.cloned.1.call-done = bf16[3072,1280]{1,0:T(8,128)(2,1)} async-done(((bf16[48,1280]{1,0:T(8,128)(2,1)}), bf16[3072,1280]{1,0:T(8,128)(2,1)}) %all-gather.5.cloned.1.call-update) | async-done | bytes 7864336 | tf_op jit(solution)/shard_map/all_gather | solution.py:454
  211.8 3.9 %fusion.10 = bf16[512,512]{1,0:T(8,128)(2,1)S(1)} fusion(bf16[3072,1280]{1,0:T(8,128)(2,1)} %all-gather.5.cloned.1.call-done, bf16[512,3072]{1,0:T(8,128)(2,1)S(1)} %copy-done.3, f32[3072]{0:T(1024)S(1)} %copy-done.7, f32[512]{0:T(512)S(1)} %add_rsqrt_fusion), kind=kOutput, calls=%fused_computation.10 | convolution fusion | flops 1617166336 | bytes 6830080 | tf_op jit(solution)/shard_map/dot_general | solution.py:462
  215.6 3.0 collective-permute-start.3
  218.6 2.5 collective-permute-start.2
  221.1 4.3 %collective-permute-start.1 = (bf16[512,512]{1,0:T(8,128)(2,1)S(1)}, bf16[512,512]{1,0:T(8,128)(2,1)S(1)}, u32[]{:S(2)}, u32[]{:S(2)}) collective-permute-start(bf16[512,512]{1,0:T(8,128)(2,1)S(1)} %fusion.10), channel_id=1, source_target_pairs={{0,12},{4,16},{8,20},{12,24},{16,28},{20,32},{24,36},{28,40},{32,4... | collective-permute-start | bytes 1572872 | tf_op jit(solution)/shard_map/ppermute | solution.py:448
  225.5 2.7 collective-permute-start
  228.2 0.0 copy-done.6
  228.2 2.7 fusion.7.q_ref
  230.9 0.0 copy-start
  230.9 0.0 copy-start.1
  231.0 48.0 %collective-permute-done = bf16[512,512]{1,0:T(8,128)(2,1)S(1)} collective-permute-done((bf16[512,512]{1,0:T(8,128)(2,1)S(1)}, bf16[512,512]{1,0:T(8,128)(2,1)S(1)}, u32[]{:S(2)}, u32[]{:S(2)}) %collective-permute-start) | collective-permute-done | bytes 524320 | tf_op jit(solution)/shard_map/ppermute | solution.py:448
  279.0 0.0 collective-permute-done.1
  279.0 0.0 collective-permute-done.2
  279.1 0.0 collective-permute-done.3
  279.2 0.0 copy-done
  279.2 0.0 copy-done.1
  279.2 0.0 copy-start.2
  279.2 21.7 %cross_attend.1 = bf16[512,768]{1,0:T(8,128)(2,1)} custom-call(s32[64]{0:T(128)S(1)} %copy-done, s32[64]{0:T(128)S(1)} %copy-done.1, bf16[512,768]{1,0:T(8,128)(2,1)S(1)} %fusion.7.q_ref, bf16[2560,512]{1,0:T(8,128)(2,1)S(1)} %constant_dynamic-update-slice_fusion.hist_ref), custom_call_target="tpu_custom_call" | custom-call | flops 12000000000 | bytes 5000000 | tf_op jit(solution)/shard_map/cross_attend/pallas_call | solution.py:432
  301.0 0.0 copy-done.2
  301.0 0.9 copy.17
  (11 shorter events, 0.2 us)
Async XLA Ops:
  7.2 77.7 %copy-start.5 = (bf16[48,512]{1,0:T(8,128)(2,1)S(1)}, bf16[48,512]{1,0:T(8,128)(2,1)}, u32[]{:S(2)}) copy-start(bf16[48,512]{1,0:T(8,128)(2,1)} %param.17) | copy-start | bytes 147460
  7.2 77.7 %copy-start.4 = (bf16[48,768]{1,0:T(8,128)(2,1)S(1)}, bf16[48,768]{1,0:T(8,128)(2,1)}, u32[]{:S(2)}) copy-start(bf16[48,768]{1,0:T(8,128)(2,1)} %param.16) | copy-start | bytes 221188
  7.2 119.8 %all-gather.3.cloned.1.call-start = ((), (), s32[]{:S(2)}) async-start(), calls=%async_computation | async-start | bytes 3932160 | tf_op jit(solution)/shard_map/all_gather | solution.py:458
  84.7 127.0 %copy-start.7 = (f32[3072]{0:T(1024)S(1)}, f32[3072]{0:T(1024)}, u32[]{:S(2)}) copy-start(f32[3072]{0:T(1024)} %param.15) | copy-start | bytes 36868
  84.8 127.0 %all-gather.5.cloned.1.call-start = ((), (), s32[]{:S(2)}) async-start(), calls=%async_computation.1 | async-start | bytes 7987200 | tf_op jit(solution)/shard_map/all_gather | solution.py:454
  127.0 84.8 %copy-start.3 = (bf16[512,3072]{1,0:T(8,128)(2,1)S(1)}, bf16[512,3072]{1,0:T(8,128)(2,1)}, u32[]{:S(2)}) copy-start(bf16[512,3072]{1,0:T(8,128)(2,1)} %all-gather.3.cloned.1.call-done) | copy-start | bytes 9437188
  211.8 16.4 %copy-start.6 = (bf16[3072,1280]{1,0:T(8,128)(2,1)S(1)}, bf16[3072,1280]{1,0:T(8,128)(2,1)}, u32[]{:S(2)}) copy-start(bf16[3072,1280]{1,0:T(8,128)(2,1)} %all-gather.5.cloned.1.call-done) | copy-start | bytes 23592964
  215.6 63.5 %collective-permute-start.3 = (bf16[512,512]{1,0:T(8,128)(2,1)S(1)}, bf16[512,512]{1,0:T(8,128)(2,1)S(1)}, u32[]{:S(2)}, u32[]{:S(2)}) collective-permute-start(bf16[512,512]{1,0:T(8,128)(2,1)S(1)} %fusion.10), channel_id=1, source_target_pairs={{0,4},{4,8},{8,12},{12,16},{16,20},{20,24},{24,28},{28,32},{32,36}... | collective-permute-start | bytes 1572872 | tf_op jit(solution)/shard_map/ppermute | solution.py:448
  218.6 60.4 %collective-permute-start.2 = (bf16[512,512]{1,0:T(8,128)(2,1)S(1)}, bf16[512,512]{1,0:T(8,128)(2,1)S(1)}, u32[]{:S(2)}, u32[]{:S(2)}) collective-permute-start(bf16[512,512]{1,0:T(8,128)(2,1)S(1)} %fusion.10), channel_id=1, source_target_pairs={{0,8},{4,12},{8,16},{12,20},{16,24},{20,28},{24,32},{28,36},{32,40... | collective-permute-start | bytes 1572872 | tf_op jit(solution)/shard_map/ppermute | solution.py:448
  221.1 57.9 %collective-permute-start.1 = (bf16[512,512]{1,0:T(8,128)(2,1)S(1)}, bf16[512,512]{1,0:T(8,128)(2,1)S(1)}, u32[]{:S(2)}, u32[]{:S(2)}) collective-permute-start(bf16[512,512]{1,0:T(8,128)(2,1)S(1)} %fusion.10), channel_id=1, source_target_pairs={{0,12},{4,16},{8,20},{12,24},{16,28},{20,32},{24,36},{28,40},{32,4... | collective-permute-start | bytes 1572872 | tf_op jit(solution)/shard_map/ppermute | solution.py:448
  225.5 53.5 %collective-permute-start = (bf16[512,512]{1,0:T(8,128)(2,1)S(1)}, bf16[512,512]{1,0:T(8,128)(2,1)S(1)}, u32[]{:S(2)}, u32[]{:S(2)}) collective-permute-start(bf16[512,512]{1,0:T(8,128)(2,1)S(1)} %fusion.10), channel_id=1, source_target_pairs={{0,16},{4,20},{8,24},{12,28},{16,32},{20,36},{24,40},{28,44},{32,4... | collective-permute-start | bytes 1572872 | tf_op jit(solution)/shard_map/ppermute | solution.py:448
  230.9 48.3 %copy-start = (s32[64]{0:T(128)S(1)}, s32[64]{0:T(128)}, u32[]{:S(2)}) copy-start(s32[64]{0:T(128)} %doc_ref.3) | copy-start | bytes 772
  230.9 48.3 %copy-start.1 = (s32[64]{0:T(128)S(1)}, s32[64]{0:T(128)}, u32[]{:S(2)}) copy-start(s32[64]{0:T(128)} %tail_ref.3) | copy-start | bytes 772
  279.2 21.7 %copy-start.2 = (bf16[512,768]{1,0:T(8,128)(2,1)S(1)}, bf16[512,768]{1,0:T(8,128)(2,1)}, u32[]{:S(2)}) copy-start(bf16[512,768]{1,0:T(8,128)(2,1)} %self_layer.1) | copy-start | bytes 2359300
Sparse Core Ops, SparseCore 0:
  84.9 42.0 all-gather.2
  130.3 81.4 all-gather.4

commit v2 on v1

--- a/solution.py
+++ b/solution.py
@@ -18,8 +18,13 @@
 HALF = WIDTH // 2
 EPSILON = 1e-06
 SCALE = 1.0 / math.sqrt(HEAD_DIM)
+EXP2_SCALE = SCALE * math.log2(math.e)
 MASKED = -1e30
+LARGE = 3.0e38
 TILE = 128
+GROUPS = 8
+SHARD = D // NBLK
+COLS = WIDTH + 2 * 2 * HEAD_DIM
 
 MESH = pl.DeviceIdType.MESH
 F32 = jnp.float32
@@ -72,6 +77,8 @@
         self.partner = (i + 1 - 2 * c, x)
         self.right = (i, (x + 1) % 4)
         self.left = (i, (x + 3) % 4)
+        self.y_up, self.y_down = (at(z, up, c), x), (at(z, down, c), x)
+        self.z_up, self.z_down = (at(z + 1, y, c), x), (at(z - 1, y, c), x)
 
 
 def greet(devices):
@@ -95,36 +102,52 @@
     return limits
 
 
-def attend_tile(q, keys, values, limits, row0, windowed):
+def flash_step(q, keys, values, limit, state, past=None):
     rows = q.shape[0]
-    query_at = row0 + lax.broadcasted_iota(jnp.int32, (rows, ROWS), 0)
-    key_at = lax.broadcasted_iota(jnp.int32, (rows, ROWS), 1)
     lane = lax.broadcasted_iota(jnp.int32, (1, ROWS), 1)
-    scores = []
-    for d in range(SLOTS):
-        s = lax.dot_general(q, keys(d), (((1,), (1,)), ((), ())), preferred_element_type=F32)
-        s = s * SCALE + jnp.where(lane < limits[d], 0.0, MASKED)
-        if d == 0:
-            s = jnp.where(key_at <= query_at, s, MASKED)
-        if d == SLOTS - 1 and windowed:
-            s = jnp.where(key_at > query_at, s, MASKED)
-        scores.append(s)
-    peak = functools.reduce(jnp.maximum, scores)
-    peak = jnp.max(peak, axis=1, keepdims=True)
-    total = None
-    blended = None
-    for d in range(SLOTS):
-        weights = jnp.exp(scores[d] - peak)
-        total = weights if total is None else total + weights
-        part = jnp.dot(weights.astype(BF16), values(d), preferred_element_type=F32)
-        blended = part if blended is None else blended + part
-    return (blended / jnp.sum(total, axis=1, keepdims=True)).astype(BF16)
+    s = lax.dot_general(q, keys, (((1,), (1,)), ((), ())), preferred_element_type=F32)
+    s = jnp.minimum(s, jnp.where(lane < limit, LARGE, MASKED))
+    if past is not None:
+        query_at = lax.broadcasted_iota(jnp.int32, (rows, ROWS), 0)
+        key_at = lax.broadcasted_iota(jnp.int32, (rows, ROWS), 1)
+        s = jnp.where(key_at <= query_at if past == "own" else key_at > query_at, s, MASKED)
+    peak = jnp.max(s, axis=1, keepdims=True)
+    if state is not None:
+        peak = jnp.maximum(peak, state[0])
+    weights = jnp.exp2((s - peak) * EXP2_SCALE)
+    total = jnp.sum(weights, axis=1, keepdims=True)
+    blended = jnp.dot(weights.astype(BF16), values, preferred_element_type=F32)
+    if state is not None:
+        shrink = jnp.exp2((state[0] - peak) * EXP2_SCALE)
+        total = state[1] * shrink + total
+        blended = state[2] * shrink + blended
+    return peak, total, blended
+
+
+def put_state(refs, h, state):
+    peak_ref, total_ref, blended_ref = refs
+    peak_ref[h] = jnp.broadcast_to(state[0], (ROWS, HEAD_DIM))
+    total_ref[h] = jnp.broadcast_to(state[1], (ROWS, HEAD_DIM))
+    blended_ref[h] = state[2]
+
+
+def get_state(refs, h):
+    peak_ref, total_ref, blended_ref = refs
+    return peak_ref[h][:, :1], total_ref[h][:, :1], blended_ref[h]
+
+
+STATE = [
+    pltpu.VMEM((HEADS, ROWS, HEAD_DIM), F32),
+    pltpu.VMEM((HEADS, ROWS, HEAD_DIM), F32),
+    pltpu.VMEM((HEADS, ROWS, HEAD_DIM), F32),
+]
 
 
 def self_kernel(
-    doc_ref, tail_ref, q_ref, res_ref, k_hbm, v_hbm, wo_hbm, hidden_ref,
-    kv, relay, ctx, woc, wrelay, acc, local_sem, send_sem, recv_sem,
+    doc_ref, tail_ref, q_ref, res_ref, shard_ref, k_hbm, v_hbm, wo_hbm, hidden_ref, wall,
+    kv, relay, ctx, woc, wrelay, acc, peak_ref, total_ref, blended_ref, local_sem, send_sem, recv_sem,
 ):
+    refs = (peak_ref, total_ref, blended_ref)
     here = Place()
     i, x, c = here.i, here.x, here.c
     copies = Copies(send_sem, recv_sem)
@@ -143,15 +166,37 @@
     own_cols = pl.ds(pl.multiple_of(x * WIDTH, WIDTH), WIDTH)
     own_w = pltpu.make_async_copy(wo_hbm.at[:, own_cols], woc.at[own_rows], local_sem.at[2 * HEADS])
     own_w.start()
+    own_shard = pltpu.make_async_copy(
+        shard_ref, wall.at[here.z, here.y, c], local_sem.at[2 * HEADS + 1]
+    )
+    own_shard.start()
 
     greet([
         here.next_chip, here.prev_chip, here.relay_to, here.relay_from, here.pass_to, here.pass_from,
-        here.partner, here.right, here.left,
+        here.partner, here.right, here.left, here.y_up, here.y_down, here.z_up, here.z_down,
     ])
 
     def go(copy):
         copy.start()
         started.append(copy)
+
+    mine = wall.at[here.z, here.y, c]
+    below = wall.at[here.z, (here.y + 3) % 4, c]
+    shard_up = copies.make("su", shard_ref, mine, here.y_up)
+    shard_down = copies.make("sd", shard_ref, mine, here.y_down)
+    shard_on = copies.make("so", below, below, here.y_up)
+
+    def group(steps):
+        return wall.at[(here.z + GROUPS + steps) % GROUPS, :, c]
+
+    def rise(n):
+        return copies.make(("rise", n), group(-n), group(-n), here.z_up)
+
+    def sink(n):
+        return copies.make(("sink", n), group(n), group(n), here.z_down)
+
+    def share(steps):
+        return copies.make(("share", steps), group(steps), group(steps), here.partner)
 
     def forth(h):
         return copies.make(("forth", h), kv.at[4, h], kv.at[1, h], here.next_chip)
@@ -217,21 +262,24 @@
 
     limits = key_limits(doc_ref, tail_ref, i)
 
-    def attend(h):
-        def slot(d):
-            return (d + SLOTS - 1) % SLOTS
-
-        def tile(t, carry):
-            row0 = pl.multiple_of(t * TILE, TILE)
-            rows = pl.ds(row0, TILE)
-            q = q_ref[rows, h * HEAD_DIM:(h + 1) * HEAD_DIM]
-            out = attend_tile(
-                q, lambda d: kv[slot(d), h, 0], lambda d: kv[slot(d), h, 1], limits, row0, True
-            )
-            ctx[rows, ctx_cols(x, h)] = out
-            return carry
-
-        lax.fori_loop(0, ROWS // TILE, tile, 0)
+    near_limit = jnp.where(c == 0, limits[1], limits[3])
+    far_limit = jnp.where(c == 0, limits[3], limits[1])
+
+    def first_keys(h):
+        q = q_ref[:, h * HEAD_DIM:(h + 1) * HEAD_DIM]
+        state = flash_step(q, kv[4, h, 0], kv[4, h, 1], limits[0], None, "own")
+        state = flash_step(q, kv[1, h, 0], kv[1, h, 1], limits[2], state)
+        near = 2 * c
+        state = flash_step(q, kv[near, h, 0], kv[near, h, 1], near_limit, state)
+        put_state(refs, h, state)
+
+    def last_keys(h):
+        q = q_ref[:, h * HEAD_DIM:(h + 1) * HEAD_DIM]
+        state = get_state(refs, h)
+        state = flash_step(q, kv[3, h, 0], kv[3, h, 1], limits[4], state, "edge")
+        far = 2 * (1 - c)
+        state = flash_step(q, kv[far, h, 0], kv[far, h, 1], far_limit, state)
+        ctx[:, ctx_cols(x, h)] = (state[2] / state[1]).astype(BF16)
         go(ctx_right(h))
         go(ctx_left(h))
 
@@ -241,6 +289,8 @@
         ctx_left(h).wait_recv()
         go(ctx_on_left(h))
 
+    go(shard_up)
+    go(shard_down)
     for h in (0, 1, 2):
         for copy in local[h]:
             copy.wait()
@@ -256,7 +306,10 @@
         for copy in local[h]:
             copy.wait()
     own_w.wait()
-
+    own_shard.wait()
+
+    shard_up.wait_recv()
+    go(shard_on)
     forth(0).wait_recv()
     go(again(0))
     go(forth(3))
@@ -264,19 +317,29 @@
     back(1).wait_recv()
     go(over(1))
     go(back(4))
+    shard_down.wait_recv()
+    shard_on.wait_recv()
+    go(rise(0))
+    go(sink(0))
+    go(share(0))
+    twin_near(0).wait_recv()
+    first_keys(0)
     forth(1).wait_recv()
     go(forth(2))
     go(twin_near(1))
     back(2).wait_recv()
     go(over(2))
     go(back(5))
+    twin_near(1).wait_recv()
+    first_keys(1)
     again(0).wait_recv()
     go(twin_far(0))
     over(1).wait_recv()
     go(twin_far(1))
-    twin_near(0).wait_recv()
     twin_far(0).wait_recv()
-    attend(0)
+    last_keys(0)
+    twin_far(1).wait_recv()
+    last_keys(1)
     w_right.wait_recv()
     go(w_twin_l)
     w_left.wait_recv()
@@ -285,9 +348,12 @@
     go(w_on_r)
     w_far_l.wait_recv()
     go(w_on_l)
-    twin_near(1).wait_recv()
-    twin_far(1).wait_recv()
-    attend(1)
+    rise(0).wait_recv()
+    go(rise(1))
+    go(share(-1))
+    sink(0).wait_recv()
+    go(sink(1))
+    go(share(1))
     forth(3).wait_recv()
     go(again(3))
     go(forth(4))
@@ -299,37 +365,52 @@
     go(twin_near(2))
     over(2).wait_recv()
     go(twin_far(2))
+    twin_near(2).wait_recv()
+    first_keys(2)
+    twin_far(2).wait_recv()
+    last_keys(2)
     w_on_r.wait_recv()
     w_on_l.wait_recv()
     go(w_twin_f)
-    twin_near(2).wait_recv()
-    twin_far(2).wait_recv()
-    attend(2)
     pass_context(0)
     pass_context(1)
+    rise(1).wait_recv()
+    go(rise(2))
+    go(share(-2))
+    sink(1).wait_recv()
+    go(sink(2))
+    go(share(2))
+    twin_near(3).wait_recv()
+    first_keys(3)
     back(5).wait_recv()
     go(over(5))
     again(3).wait_recv()
     go(twin_far(3))
-    twin_near(3).wait_recv()
     twin_far(3).wait_recv()
-    attend(3)
+    last_keys(3)
     pass_context(2)
     forth(4).wait_recv()
     go(twin_near(4))
+    twin_near(4).wait_recv()
+    first_keys(4)
     over(4).wait_recv()
     go(twin_far(4))
-    twin_near(4).wait_recv()
     twin_far(4).wait_recv()
-    attend(4)
+    last_keys(4)
     pass_context(3)
+    rise(2).wait_recv()
+    go(rise(3))
+    go(share(-3))
+    sink(2).wait_recv()
+    go(share(3))
     forth(5).wait_recv()
     go(twin_near(5))
+    twin_near(5).wait_recv()
+    first_keys(5)
     over(5).wait_recv()
     go(twin_far(5))
-    twin_near(5).wait_recv()
     twin_far(5).wait_recv()
-    attend(5)
+    last_keys(5)
     pass_context(4)
     for copy in (w_twin_l, w_twin_r, w_twin_f):
         copy.wait_recv()
@@ -363,22 +444,30 @@
         ctx_on_right(h).wait_recv()
         ctx_on_left(h).wait_recv()
     project(4 * HEAD_DIM, 2 * HEAD_DIM, lambda rows: acc[rows, :], finish)
+    rise(3).wait_recv()
+    go(share(-4))
+    for steps in range(-4, 4):
+        share(steps).wait_recv()
     for copy in started:
         copy.wait_send()
-
-
-N_SELF = 62
-
-
-def self_layer(doc, tail, q, res, k, v, wo):
+    assert len(copies.made) == N_SELF
+
+
+N_SELF = 79
+
+
+def self_layer(doc, tail, q, res, shard, k, v, wo):
     any_spec = pl.BlockSpec(memory_space=pl.ANY)
     vmem = pl.BlockSpec(memory_space=pltpu.VMEM)
     smem = pl.BlockSpec(memory_space=pltpu.SMEM)
     return pl.pallas_call(
         self_kernel,
-        out_shape=jax.ShapeDtypeStruct((ROWS, WIDTH), BF16),
-        in_specs=[smem, smem, vmem, vmem, any_spec, any_spec, any_spec],
-        out_specs=vmem,
+        out_shape=(
+            jax.ShapeDtypeStruct((ROWS, WIDTH), BF16),
+            jax.ShapeDtypeStruct((GROUPS, 4, 2, SHARD, COLS), BF16),
+        ),
+        in_specs=[smem, smem, vmem, vmem, vmem, any_spec, any_spec, any_spec],
+        out_specs=(vmem, any_spec),
         scratch_shapes=[
             pltpu.VMEM((SLOTS, HEADS, 2, ROWS, HEAD_DIM), BF16),
             pltpu.VMEM((len(MINUS), 2, ROWS, HEAD_DIM), BF16),
@@ -386,7 +475,8 @@
             pltpu.VMEM((D, WIDTH), BF16),
             pltpu.VMEM((2, HALF // 2, WIDTH), BF16),
             pltpu.VMEM((ROWS, WIDTH), F32),
-            pltpu.SemaphoreType.DMA((2 * HEADS + 1,)),
+            *STATE,
+            pltpu.SemaphoreType.DMA((2 * HEADS + 2,)),
             pltpu.SemaphoreType.DMA((N_SELF,)),
             pltpu.SemaphoreType.DMA((N_SELF,)),
         ],
@@ -397,73 +487,227 @@
             flops=60_000_000_000, bytes_accessed=20_000_000, transcendentals=0
         ),
         name="self_layer",
-    )(doc, tail, q, res, k, v, wo)
-
-
-def cross_kernel(doc_ref, tail_ref, q_ref, hist_ref, out_ref):
-    i = lax.axis_index("seq")
+    )(doc, tail, q, res, shard, k, v, wo)
+
+
+PARTS = ROWS // TILE
+CACHE = 2 * 2 * HEAD_DIM
+CACHE_PLUS = (0, 2)
+CACHE_MINUS = (1, 3)
+
+
+def cross_kernel(
+    doc_ref, tail_ref, gain_ref, hidden_hbm, wall_hbm, out_ref,
+    hid, wall, cache, relay, queries, peak_ref, total_ref, blended_ref, local_sem, send_sem, recv_sem,
+):
+    refs = (peak_ref, total_ref, blended_ref)
+    here = Place()
+    i, x, c = here.i, here.x, here.c
+    copies = Copies(send_sem, recv_sem)
+    started = []
+    left_x, right_x = (x + 3) % 4, (x + 1) % 4
+
+    def cols(block):
+        return pl.ds(pl.multiple_of(block * WIDTH, WIDTH), WIDTH)
+
+    own = pltpu.make_async_copy(hidden_hbm, hid.at[:, cols(x)], local_sem.at[0])
+    own.start()
+    load = pltpu.make_async_copy(wall_hbm, wall, local_sem.at[1])
+    load.start()
+    greet([
+        here.next_chip, here.prev_chip, here.relay_to, here.relay_from, here.pass_to, here.pass_from,
+        here.partner, here.right, here.left,
+    ])
+
+    def go(copy):
+        copy.start()
+        started.append(copy)
+
+    def rows(r):
+        return pl.ds(r * TILE, TILE)
+
+    def to_right(r):
+        part = hid.at[rows(r), cols(x)]
+        return copies.make(("r", r), part, part, here.right)
+
+    def to_left(r):
+        part = hid.at[rows(r), cols(x)]
+        return copies.make(("l", r), part, part, here.left)
+
+    def on_right(r):
+        part = hid.at[pl.ds(r * TILE, TILE // 2), cols(left_x)]
+        return copies.make(("or", r), part, part, here.right)
+
+    def on_left(r):
+        part = hid.at[pl.ds(r * TILE + TILE // 2, TILE // 2), cols(right_x)]
+        return copies.make(("ol", r), part, part, here.left)
+
+    def forth(r):
+        return copies.make(("forth", r), cache.at[4, rows(r)], cache.at[1, rows(r)], here.next_chip)
+
+    def again(r):
+        return copies.make(("again", r), cache.at[1, rows(r)], cache.at[3, rows(r)], here.next_chip)
+
+    def back(r):
+        return copies.make(("back", r), cache.at[4, rows(r)], relay.at[CACHE_MINUS.index(r)], here.relay_to)
+
+    def over(r):
+        return copies.make(("over", r), relay.at[CACHE_MINUS.index(r)], cache.at[3, rows(r)], here.pass_to)
+
+    def twin_near(r):
+        return copies.make(("near", r), cache.at[1, rows(r)], cache.at[2 * (1 - c), rows(r)], here.partner)
+
+    def twin_far(r):
+        return copies.make(("far", r), cache.at[4 - c, rows(r)], cache.at[2 * c, rows(r)], here.partner)
+
+    def hand_on(r):
+        to_right(r).wait_recv()
+        go(on_right(r))
+        to_left(r).wait_recv()
+        go(on_left(r))
+
+    def make_part(r):
+        on_right(r).wait_recv()
+        on_left(r).wait_recv()
+        wide = hid[r * TILE:(r + 1) * TILE, :].astype(F32)
+        mean_square = jnp.sum(wide * wide, axis=1, keepdims=True) / D
+        normed = (wide * lax.rsqrt(mean_square + EPSILON) * gain_ref[...]).astype(BF16)
+        made = jnp.dot(normed, wall[:, WIDTH:], preferred_element_type=F32).astype(BF16)
+        cache[4, r * TILE:(r + 1) * TILE, :] = made
+        asked = jnp.dot(normed, wall[:, :WIDTH], preferred_element_type=F32).astype(BF16)
+        queries[r * TILE:(r + 1) * TILE, :] = asked
+        go(forth(r))
+        if r in CACHE_MINUS:
+            go(back(r))
+
+    def arrive(r):
+        forth(r).wait_recv()
+        go(twin_near(r))
+        if r in CACHE_PLUS:
+            go(again(r))
+        else:
+            back(r).wait_recv()
+            go(over(r))
+
+    def finish(r):
+        (again if r in CACHE_PLUS else over)(r).wait_recv()
+        go(twin_far(r))
+
+    own.wait()
+    for r in (0, 1):
+        go(to_right(r))
+        go(to_left(r))
+    hand_on(0)
+    go(to_right(2))
+    go(to_left(2))
+    load.wait()
+    hand_on(1)
+    go(to_right(3))
+    go(to_left(3))
+    make_part(0)
+    hand_on(2)
+    make_part(1)
+    arrive(0)
+    hand_on(3)
+    make_part(2)
+    arrive(1)
+    finish(0)
+    make_part(3)
+    arrive(2)
+    finish(1)
+
     limits = key_limits(doc_ref, tail_ref, i)
-
-    def slot_rows(d):
-        at = (SLOTS - 1 - d) * ROWS
-        return slice(at, at + ROWS)
-
-    for h in range(HEADS):
+    near_limit = jnp.where(c == 0, limits[1], limits[3])
+    far_limit = jnp.where(c == 0, limits[3], limits[1])
+
+    def head_cols(h):
+        return pl.ds(pl.multiple_of(h * HEAD_DIM, HEAD_DIM), HEAD_DIM)
+
+    def step(h, slot, limit, state, past=None):
         g = h // 3
-
-        def tile(t, carry):
-            row0 = pl.multiple_of(t * TILE, TILE)
-            rows = pl.ds(row0, TILE)
-            q = q_ref[rows, h * HEAD_DIM:(h + 1) * HEAD_DIM]
-            out_ref[rows, h * HEAD_DIM:(h + 1) * HEAD_DIM] = attend_tile(
-                q,
-                lambda d: hist_ref[slot_rows(d), g * HEAD_DIM:(g + 1) * HEAD_DIM],
-                lambda d: hist_ref[slot_rows(d), (2 + g) * HEAD_DIM:(3 + g) * HEAD_DIM],
-                limits, row0, False,
-            )
-            return carry
-
-        lax.fori_loop(0, ROWS // TILE, tile, 0)
-
-
-def cross_attend(doc, tail, q, hist):
+        return flash_step(
+            queries[:, head_cols(h)],
+            cache[slot, :, head_cols(g)],
+            cache[slot, :, head_cols(g + 2)],
+            limit, state, past,
+        )
+
+    def own_keys(h, carry):
+        put_state(refs, h, step(h, 4, limits[0], None, "own"))
+        return carry
+
+    lax.fori_loop(0, HEADS, own_keys, 0)
+    arrive(3)
+    finish(2)
+    for r in range(PARTS):
+        twin_near(r).wait_recv()
+
+    def near_keys(h, carry):
+        state = step(h, 1, limits[2], get_state(refs, h))
+        put_state(refs, h, step(h, 2 * c, near_limit, state))
+        return carry
+
+    lax.fori_loop(0, HEADS, near_keys, 0)
+    finish(3)
+    for r in range(PARTS):
+        twin_far(r).wait_recv()
+
+    def far_keys(h, carry):
+        state = step(h, 3, limits[4], get_state(refs, h))
+        state = step(h, 2 * (1 - c), far_limit, state)
+        out_ref[:, head_cols(h)] = (state[2] / state[1]).astype(BF16)
+        return carry
+
+    lax.fori_loop(0, HEADS, far_keys, 0)
+    for copy in started:
+        copy.wait_send()
+    assert len(copies.made) == N_CROSS
+
+
+N_CROSS = 34
+
+
+def cross_layer(doc, tail, gain, hidden, wall):
+    any_spec = pl.BlockSpec(memory_space=pl.ANY)
     vmem = pl.BlockSpec(memory_space=pltpu.VMEM)
     smem = pl.BlockSpec(memory_space=pltpu.SMEM)
     return pl.pallas_call(
         cross_kernel,
         out_shape=jax.ShapeDtypeStruct((ROWS, WIDTH), BF16),
-        in_specs=[smem, smem, vmem, vmem],
+        in_specs=[smem, smem, vmem, any_spec, any_spec],
         out_specs=vmem,
-        compiler_params=pltpu.CompilerParams(vmem_limit_bytes=48 * 1024 * 1024),
+        scratch_shapes=[
+            pltpu.VMEM((ROWS, D), BF16),
+            pltpu.VMEM((D, COLS), BF16),
+            pltpu.VMEM((SLOTS, ROWS, CACHE), BF16),
+            pltpu.VMEM((len(CACHE_MINUS), TILE, CACHE), BF16),
+            pltpu.VMEM((ROWS, WIDTH), BF16),
+            *STATE,
+            pltpu.SemaphoreType.DMA((2,)),
+            pltpu.SemaphoreType.DMA((N_CROSS,)),
+            pltpu.SemaphoreType.DMA((N_CROSS,)),
+        ],
+        compiler_params=pltpu.CompilerParams(
+            collective_id=1, has_side_effects=True, vmem_limit_bytes=56 * 1024 * 1024
+        ),
         cost_estimate=pl.CostEstimate(
-            flops=12_000_000_000, bytes_accessed=5_000_000, transcendentals=0
+            flops=60_000_000_000, bytes_accessed=20_000_000, transcendentals=0
         ),
-        name="cross_attend",
-    )(doc, tail, q, hist)
-
-
-def passed_along(block, axis, distance):
-    devices = range(lax.axis_size(axis))
-    route = [(i - distance, i) for i in devices if i - distance in devices]
-    return lax.ppermute(block, axis, route)
+        name="cross_layer",
+    )(doc, tail, gain, hidden, wall)
 
 
 def local(
     residual, q_self, k_self, v_self, w_out, norm_gain, w_query, w_cache, block_doc, tail_len
 ):
-    weights = lax.all_gather(
-        jnp.concatenate([w_query, w_cache], axis=1), "seq", axis=0, tiled=True
+    shard = jnp.concatenate([w_query, w_cache], axis=1)
+    hidden, wall = self_layer(
+        block_doc, tail_len, q_self, residual, shard, k_self, v_self, w_out
     )
-    hidden = self_layer(block_doc, tail_len, q_self, residual, k_self, v_self, w_out)
-    everything = lax.all_gather(hidden, "head", axis=1, tiled=True)
-    wide = everything.astype(F32)
-    mean_square = jnp.mean(wide * wide, axis=1, keepdims=True)
-    normed = (wide * lax.rsqrt(mean_square + EPSILON) * norm_gain).astype(BF16)
-    cache_rows = jnp.dot(normed, weights[:, WIDTH:], preferred_element_type=F32).astype(BF16)
-    cross_queries = jnp.dot(normed, weights[:, :WIDTH], preferred_element_type=F32).astype(BF16)
-    earlier = [passed_along(cache_rows, "seq", offset) for offset in range(SLOTS - 1, 0, -1)]
-    history = jnp.concatenate(earlier + [cache_rows], axis=0)
-    return (hidden, cross_attend(block_doc, tail_len, cross_queries, history))
+    cross = cross_layer(
+        block_doc, tail_len, norm_gain.reshape(1, D), hidden, wall.reshape(D, COLS)
+    )
+    return (hidden, cross)
 
 
 def solution(mesh):

time: 309 us -> 200 us (0.65)
  the two profiles are of different devices: /device:TPU:41 before, /device:TPU:9 now
where the time goes in v2:
time: 200 us; the launch traced here: 197 us
  Pallas kernels  192 us (96%)
  local copies, waits for them, and re-layouts  2.95 us (1%)
    pallas_call x1, Pallas kernels, self_layer(): pl.pallas_call(self_kernel, out_shape=(jax.ShapeDtypeStruct((ROWS, WIDTH)...  109 us
    pallas_call x1, Pallas kernels, cross_layer(): pl.pallas_call(cross_kernel, out_shape=jax.ShapeDtypeStruct((ROWS, WIDTH)...  83.5 us

profile of v2, /device:TPU:9, one launch (start us, length us, event | category | flops | bytes accessed | tf_op | source)
XLA Modules:
  0.0 197.3 jit_solution(11800197388782392615)
XLA Ops:
  0.6 1.6 pad_maximum_fusion.shard_ref
  2.2 108.7 %self_layer.1 = (bf16[512,768]{1,0:T(8,128)(2,1)}, bf16[8,4,2,48,1280]{4,3,2,1,0:T(8,128)(2,1)}) custom-call(s32[64]{0:T(128)} %doc_ref.3, s32[64]{0:T(128)} %tail_ref.3, bf16[512,768]{1,0:T(8,128)(2,1)} %q_ref.1, bf16[512,768]{1,0:T(8,128)(2,1)} %res_ref.1, bf16[48,1280]{1,0:T(8,128)(2,1)} %pad_maximum_fusion.shard_ref, bf16[512,768]{1,0:T(8,128)(2,1)} %k_hbm.1, ...), custom_call_target="tpu_custom_call" | custom-call | flops 60000002048 | bytes 20000000 | tf_op jit(solution)/shard_map/self_layer/pallas_call | solution.py:463
  110.9 0.0 copy-start
  110.9 83.5 %cross_layer.1 = bf16[512,768]{1,0:T(8,128)(2,1)} custom-call(s32[64]{0:T(128)} %doc_ref.3, s32[64]{0:T(128)} %tail_ref.3, f32[1,3072]{1,0:T(1,128)} %bitcast.2, bf16[512,768]{1,0:T(8,128)(2,1)} %get-tuple-element.8.hidden_hbm, bf16[3072,1280]{1,0:T(8,128)(2,1)} %bitcast.3), custom_call_target="tpu_custom_call" | custom-call | flops 60000002048 | bytes 20000000 | tf_op jit(solution)/shard_map/cross_layer/pallas_call | solution.py:674
  194.4 0.0 copy-done
  194.4 0.9 copy.14
  195.2 2.1 %copy.15 = bf16[512,768]{1,0:T(8,128)(2,1)} copy(bf16[512,768]{1,0:T(8,128)(2,1)} %cross_layer.1) | data formatting | bytes 1572864
Async XLA Ops:
  110.9 83.5 %copy-start = (bf16[512,768]{1,0:T(8,128)(2,1)S(1)}, bf16[512,768]{1,0:T(8,128)(2,1)}, u32[]{:S(2)}) copy-start(bf16[512,768]{1,0:T(8,128)(2,1)} %get-tuple-element.8.hidden_hbm) | copy-start | bytes 2359300

commit v3 on v2

v3 whole, which is shorter than its diff:
```python
import functools
import math

import jax
import jax.numpy as jnp
from jax import lax
from jax.experimental import pallas as pl
from jax.experimental.pallas import tpu as pltpu
from jax.sharding import PartitionSpec as P

D = 3072
HEAD_DIM = 128
ROWS = 512
NBLK = 64
HEADS = 6
SLOTS = 5
WIDTH = HEADS * HEAD_DIM
HALF = WIDTH // 2
EPSILON = 1e-06
SCALE = 1.0 / math.sqrt(HEAD_DIM)
EXP2_SCALE = SCALE * math.log2(math.e)
MASKED = -1e30
LARGE = 3.0e38
TILE = 128
GROUPS = 8
SHARD = D // NBLK
COLS = WIDTH + 2 * 2 * HEAD_DIM

MESH = pl.DeviceIdType.MESH
F32 = jnp.float32
BF16 = jnp.bfloat16

PLUS = (0, 3)
MINUS = (1, 2, 4, 5)


PARTS = ROWS // TILE
CACHE = 2 * 2 * HEAD_DIM
CACHE_PLUS = (0, 2)
CACHE_MINUS = (1, 3)


class Copies:
    def __init__(self, send_sem, recv_sem):
        self.send_sem, self.recv_sem = send_sem, recv_sem
        self.made = {}

    def make(self, name, src, dst, device):
        if name not in self.made:
            self.made[name] = len(self.made)
        n = self.made[name]
        return pltpu.make_async_remote_copy(
            src_ref=src,
            dst_ref=dst,
            send_sem=self.send_sem.at[n],
            recv_sem=self.recv_sem.at[n],
            device_id=device,
            device_id_type=MESH,
        )


class Place:
    def __init__(self):
        i = lax.axis_index("seq")
        x = lax.axis_index("head")
        self.i, self.x = i, x
        c = i % 2
        y = (i // 2) % 4
        z = i // 8
        self.c, self.y, self.z = c, y, z

        def at(zz, yy, cc):
            return ((zz + 8) % 8 * 4 + yy) * 2 + cc

        up = (y + 1) % 4
        down = (y + 3) % 4
        self.next_chip = (at(z + (y + 1) // 4, up, c), x)
        self.prev_chip = (at(z - (6 - y) // 6, down, c), x)
        self.relay_to = (at(z, down, c), x)
        self.relay_from = (at(z, up, c), x)
        self.pass_to = (at(z + (up + 2) // 4, down, c), x)
        self.pass_from = (at(z - ((y + 2) % 4) // 2, up, c), x)
        self.partner = (i + 1 - 2 * c, x)
        self.right = (i, (x + 1) % 4)
        self.left = (i, (x + 3) % 4)
        self.y_up, self.y_down = (at(z, up, c), x), (at(z, down, c), x)
        self.y_far = (at(z, (y + 2) % 4, c), x)
        self.z_up, self.z_down = (at(z + 1, y, c), x), (at(z - 1, y, c), x)


def greet(devices):
    barrier = pltpu.get_barrier_semaphore()
    for device in devices:
        pl.semaphore_signal(barrier, inc=1, device_id=device, device_id_type=MESH)
    pl.semaphore_wait(barrier, len(devices))


def key_limits(doc_ref, tail_ref, i):
    limits = []
    own = doc_ref[i]
    for d in range(SLOTS):
        j = jnp.maximum(i - d, 0)
        doc = doc_ref[j]
        after = doc_ref[jnp.minimum(j + 1, NBLK - 1)]
        closing = jnp.logical_or(j == NBLK - 1, after != doc)
        count = jnp.where(closing, tail_ref[j], ROWS)
        seen = jnp.logical_and(i - d >= 0, doc == own)
        limits.append(jnp.where(seen, count, 0))
    return limits


def flash_step(q, keys, values, limit, state, past=None):
    rows = q.shape[0]
    lane = lax.broadcasted_iota(jnp.int32, (1, ROWS), 1)
    s = lax.dot_general(q, keys, (((1,), (1,)), ((), ())), preferred_element_type=F32)
    s = jnp.minimum(s, jnp.where(lane < limit, LARGE, MASKED))
    if past is not None:
        query_at = lax.broadcasted_iota(jnp.int32, (rows, ROWS), 0)
        key_at = lax.broadcasted_iota(jnp.int32, (rows, ROWS), 1)
        s = jnp.where(key_at <= query_at if past == "own" else key_at > query_at, s, MASKED)
    peak = jnp.max(s, axis=1, keepdims=True)
    if state is not None:
        peak = jnp.maximum(peak, state[0])
    spread = peak if peak.shape[1] == 1 else jnp.concatenate([peak] * (ROWS // HEAD_DIM), axis=1)
    weights = jnp.exp2((s - spread) * EXP2_SCALE)
    total = jnp.sum(weights, axis=1, keepdims=True)
    blended = jnp.dot(weights.astype(BF16), values, preferred_element_type=F32)
    if state is not None:
        shrink = jnp.exp2((state[0] - peak) * EXP2_SCALE)
        total = state[1] * shrink + total
        blended = state[2] * shrink + blended
    return peak, total, blended


def put_state(refs, h, state):
    peak_ref, total_ref, blended_ref = refs
    peak_ref[h] = jnp.broadcast_to(state[0], (ROWS, HEAD_DIM))
    total_ref[h] = jnp.broadcast_to(state[1], (ROWS, HEAD_DIM))
    blended_ref[h] = state[2]


def get_state(refs, h):
    peak_ref, total_ref, blended_ref = refs
    return peak_ref[h], total_ref[h], blended_ref[h]


STATE = [
    pltpu.VMEM((HEADS, ROWS, HEAD_DIM), F32),
    pltpu.VMEM((HEADS, ROWS, HEAD_DIM), F32),
    pltpu.VMEM((HEADS, ROWS, HEAD_DIM), F32),
]


def layer_kernel(
    doc_ref, tail_ref, q_ref, res_ref, gain_ref, k_hbm, v_hbm, wo_hbm, wq_hbm, wc_hbm,
    hidden_ref, out_ref,
    kv, relay, ctx, woc, wrelay, acc, peak_ref, total_ref, blended_ref,
    hid, wall, cache, crelay, queries, local_sem, send_sem, recv_sem,
):
    refs = (peak_ref, total_ref, blended_ref)
    here = Place()
    i, x, c = here.i, here.x, here.c
    copies = Copies(send_sem, recv_sem)
    started = []
    right_x, left_x, far_x = (x + 1) % 4, (x + 3) % 4, (x + 2) % 4

    local = []
    for h in range(HEADS):
        cols = pl.ds(h * HEAD_DIM, HEAD_DIM)
        one = pltpu.make_async_copy(k_hbm.at[:, cols], kv.at[SLOTS - 1, h, 0], local_sem.at[2 * h])
        two = pltpu.make_async_copy(v_hbm.at[:, cols], kv.at[SLOTS - 1, h, 1], local_sem.at[2 * h + 1])
        one.start()
        two.start()
        local.append((one, two))
    own_rows = pl.ds(pl.multiple_of(x * WIDTH, WIDTH), WIDTH)
    own_cols = pl.ds(pl.multiple_of(x * WIDTH, WIDTH), WIDTH)
    own_w = pltpu.make_async_copy(wo_hbm.at[:, own_cols], woc.at[own_rows], local_sem.at[2 * HEADS])
    own_w.start()
    shard = wall.at[here.z, here.y, c]
    shard_loads = (
        pltpu.make_async_copy(wq_hbm, shard.at[:, pl.ds(0, WIDTH)], local_sem.at[2 * HEADS + 1]),
        pltpu.make_async_copy(wc_hbm, shard.at[:, pl.ds(WIDTH, CACHE)], local_sem.at[2 * HEADS + 2]),
    )
    for copy in shard_loads:
        copy.start()

    greet([
        here.next_chip, here.prev_chip, here.relay_to, here.relay_from, here.pass_to, here.pass_from,
        here.partner, here.right, here.left, here.y_up, here.y_down, here.y_far, here.y_far, here.z_up, here.z_down,
    ])

    def go(copy):
        copy.start()
        started.append(copy)

    shard_up = copies.make("su", shard, shard, here.y_up)
    shard_down = copies.make("sd", shard, shard, here.y_down)
    shard_far = copies.make("sf", shard, shard, here.y_far)

    def group(steps, part):
        return wall.at[(here.z + GROUPS + steps) % GROUPS, pl.ds(2 * part, 2), c]

    def rise(n, part):
        return copies.make(("rise", n, part), group(-n, part), group(-n, part), here.z_up)

    def sink(n, part):
        return copies.make(("sink", n, part), group(n, part), group(n, part), here.z_down)

    def share(steps, part):
        return copies.make(("share", steps, part), group(steps, part), group(steps, part), here.partner)

    def forth(h):
        return copies.make(("forth", h), kv.at[4, h], kv.at[1, h], here.next_chip)

    def again(h):
        return copies.make(("again", h), kv.at[1, h], kv.at[3, h], here.next_chip)

    def back(h):
        return copies.make(("back", h), kv.at[4, h], relay.at[MINUS.index(h)], here.relay_to)

    def over(h):
        return copies.make(("over", h), relay.at[MINUS.index(h)], kv.at[3, h], here.pass_to)

    def twin_near(h):
        return copies.make(("near", h), kv.at[1, h], kv.at[2 * (1 - c), h], here.partner)

    def twin_far(h):
        return copies.make(("far", h), kv.at[4 - c, h], kv.at[2 * c, h], here.partner)

    def w_rows(block, first, count):
        return pl.ds(pl.multiple_of(block * WIDTH + c * HALF + first, 64), count)

    def w_cols(block):
        return pl.ds(pl.multiple_of(block * WIDTH, WIDTH), WIDTH)

    quarter = HALF // 2
    c_half = pl.ds(pl.multiple_of(c * HALF, HALF), HALF)
    c_one = pl.ds(pl.multiple_of(c * HALF, 64), quarter)
    c_two = pl.ds(pl.multiple_of(c * HALF + quarter, 64), quarter)
    w_right = copies.make("wr", wo_hbm.at[c_half, w_cols(right_x)], woc.at[w_rows(x, 0, HALF)], here.right)
    w_left = copies.make("wl", wo_hbm.at[c_half, w_cols(left_x)], woc.at[w_rows(x, 0, HALF)], here.left)
    w_far_r = copies.make("wfr", wo_hbm.at[c_one, w_cols(far_x)], wrelay.at[0], here.right)
    w_far_l = copies.make("wfl", wo_hbm.at[c_two, w_cols(far_x)], wrelay.at[1], here.left)
    w_on_r = copies.make("wor", wrelay.at[0], woc.at[w_rows(left_x, 0, quarter)], here.right)
    w_on_l = copies.make("wol", wrelay.at[1], woc.at[w_rows(right_x, quarter, quarter)], here.left)

    def w_twin(name, block):
        rows = w_rows(block, 0, HALF)
        return copies.make(("wt", name), woc.at[rows], woc.at[rows], here.partner)

    w_twin_l = w_twin("l", left_x)
    w_twin_r = w_twin("r", right_x)
    w_twin_f = w_twin("f", far_x)

    def ctx_cols(block, h):
        return pl.ds(pl.multiple_of(block * WIDTH + h * HEAD_DIM, HEAD_DIM), HEAD_DIM)

    upper, lower = pl.ds(0, ROWS // 2), pl.ds(ROWS // 2, ROWS // 2)

    def ctx_right(h):
        return copies.make(("cr", h), ctx.at[:, ctx_cols(x, h)], ctx.at[:, ctx_cols(x, h)], here.right)

    def ctx_left(h):
        return copies.make(("cl", h), ctx.at[:, ctx_cols(x, h)], ctx.at[:, ctx_cols(x, h)], here.left)

    def ctx_on_right(h):
        part = ctx.at[upper, ctx_cols(left_x, h)]
        return copies.make(("cor", h), part, part, here.right)

    def ctx_on_left(h):
        part = ctx.at[lower, ctx_cols(right_x, h)]
        return copies.make(("col", h), part, part, here.left)

    limits = key_limits(doc_ref, tail_ref, i)

    near_limit = jnp.where(c == 0, limits[1], limits[3])
    far_limit = jnp.where(c == 0, limits[3], limits[1])

    def first_keys(h):
        q = q_ref[:, h * HEAD_DIM:(h + 1) * HEAD_DIM]
        state = flash_step(q, kv[4, h, 0], kv[4, h, 1], limits[0], None, "own")
        state = flash_step(q, kv[1, h, 0], kv[1, h, 1], limits[2], state)
        near = 2 * c
        state = flash_step(q, kv[near, h, 0], kv[near, h, 1], near_limit, state)
        put_state(refs, h, state)

    def last_keys(h):
        q = q_ref[:, h * HEAD_DIM:(h + 1) * HEAD_DIM]
        state = get_state(refs, h)
        state = flash_step(q, kv[3, h, 0], kv[3, h, 1], limits[4], state, "edge")
        far = 2 * (1 - c)
        state = flash_step(q, kv[far, h, 0], kv[far, h, 1], far_limit, state)
        ctx[:, ctx_cols(x, h)] = (state[2] / state[1]).astype(BF16)
        go(ctx_right(h))
        go(ctx_left(h))

    def pass_context(h):
        ctx_right(h).wait_recv()
        go(ctx_on_right(h))
        ctx_left(h).wait_recv()
        go(ctx_on_left(h))

    def sunk(n, part, last=False):
        sink(n, part).wait_recv()
        if not last:
            go(sink(n + 1, part))
        go(share(n + 1, part))

    def risen(n, part, last=False):
        rise(n, part).wait_recv()
        if not last:
            go(rise(n + 1, part))
        go(share(-n - 1, part))

    for copy in shard_loads:
        copy.wait()
    go(shard_up)
    go(shard_down)
    go(shard_far)
    for h in (0, 1, 2):
        for copy in local[h]:
            copy.wait()
    go(forth(0))
    go(back(1))
    go(w_right)
    go(w_left)
    go(w_far_r)
    go(w_far_l)
    go(forth(1))
    go(back(2))
    for h in (3, 4, 5):
        for copy in local[h]:
            copy.wait()
    own_w.wait()

    shard_up.wait_recv()
    shard_down.wait_recv()
    shard_far.wait_recv()
    for part in (0, 1):
        go(sink(0, part))
        go(share(0, part))
    back(1).wait_recv()
    go(over(1))
    go(back(4))
    forth(0).wait_recv()
    go(again(0))
    go(forth(3))
    go(twin_near(0))
    twin_near(0).wait_recv()
    first_keys(0)
    sunk(0, 0)
    back(2).wait_recv()
    go(over(2))
    go(back(5))
    forth(1).wait_recv()
    go(forth(2))
    go(twin_near(1))
    twin_near(1).wait_recv()
    first_keys(1)
    sunk(0, 1)
    w_right.wait_recv()
    go(w_twin_l)
    w_left.wait_recv()
    go(w_twin_r)
    w_far_r.wait_recv()
    go(w_on_r)
    w_far_l.wait_recv()
    go(w_on_l)
    over(1).wait_recv()
    go(twin_far(1))
    again(0).wait_recv()
    go(twin_far(0))
    twin_far(1).wait_recv()
    last_keys(1)
    twin_far(0).wait_recv()
    last_keys(0)
    sunk(1, 0)
    back(4).wait_recv()
    go(over(4))
    forth(3).wait_recv()
    go(again(3))
    go(forth(4))
    go(forth(5))
    go(twin_near(3))
    sunk(1, 1)
    w_on_r.wait_recv()
    w_on_l.wait_recv()
    go(w_twin_f)
    twin_near(3).wait_recv()
    first_keys(3)
    over(2).wait_recv()
    go(twin_far(2))
    forth(2).wait_recv()
    go(twin_near(2))
    pass_context(1)
    pass_context(0)
    twin_near(2).wait_recv()
    first_keys(2)
    twin_far(2).wait_recv()
    last_keys(2)
    back(5).wait_recv()
    go(over(5))
    sunk(2, 0)
    again(3).wait_recv()
    go(twin_far(3))
    sunk(2, 1)
    twin_far(3).wait_recv()
    last_keys(3)
    pass_context(2)
    over(4).wait_recv()
    go(twin_far(4))
    forth(4).wait_recv()
    go(twin_near(4))
    for part in (0, 1):
        go(rise(0, part))
    twin_near(4).wait_recv()
    first_keys(4)
    twin_far(4).wait_recv()
    last_keys(4)
    sunk(3, 0)
    pass_context(3)
    over(5).wait_recv()
    go(twin_far(5))
    forth(5).wait_recv()
    go(twin_near(5))
    twin_near(5).wait_recv()
    first_keys(5)
    twin_far(5).wait_recv()
    last_keys(5)
    sunk(3, 1)
    pass_context(4)
    for copy in (w_twin_l, w_twin_r, w_twin_f):
        copy.wait_recv()
    for h in range(4):
        ctx_on_right(h).wait_recv()
        ctx_on_left(h).wait_recv()

    def project(first, count, seed, store):
        def tile(t, carry):
            rows = pl.ds(pl.multiple_of(t * TILE, TILE), TILE)
            total = seed(rows)
            for block in range(4):
                at = block * WIDTH + first
                total = total + jnp.dot(
                    ctx[rows, at:at + count], woc[at:at + count, :], preferred_element_type=F32
                )
            store(rows, total)
            return carry

        lax.fori_loop(0, ROWS // TILE, tile, 0)

    def keep(rows, total):
        acc[rows, :] = total

    def cols(block):
        return pl.ds(pl.multiple_of(block * WIDTH, WIDTH), WIDTH)

    def finish(rows, total):
        tile = (res_ref[rows, :].astype(F32) + total).astype(BF16)
        hidden_ref[rows, :] = tile
        hid[rows, cols(x)] = tile

    project(0, 4 * HEAD_DIM, lambda rows: jnp.zeros((TILE, WIDTH), F32), keep)
    pass_context(5)
    for h in (4, 5):
        ctx_on_right(h).wait_recv()
        ctx_on_left(h).wait_recv()
    project(4 * HEAD_DIM, 2 * HEAD_DIM, lambda rows: acc[rows, :], finish)

    def part_rows(r):
        return pl.ds(r * TILE, TILE)

    def to_right(r):
        part = hid.at[part_rows(r), cols(x)]
        return copies.make(("r", r), part, part, here.right)

    def to_left(r):
        part = hid.at[part_rows(r), cols(x)]
        return copies.make(("l", r), part, part, here.left)

    def on_right(r):
        part = hid.at[pl.ds(r * TILE, TILE // 2), cols(left_x)]
        return copies.make(("or", r), part, part, here.right)

    def on_left(r):
        part = hid.at[pl.ds(r * TILE + TILE // 2, TILE // 2), cols(right_x)]
        return copies.make(("ol", r), part, part, here.left)

    def c_forth(r):
        return copies.make(("c_forth", r), cache.at[4, part_rows(r)], cache.at[1, part_rows(r)], here.next_chip)

    def c_again(r):
        return copies.make(("c_again", r), cache.at[1, part_rows(r)], cache.at[3, part_rows(r)], here.next_chip)

    def c_back(r):
        return copies.make(("c_back", r), cache.at[4, part_rows(r)], crelay.at[CACHE_MINUS.index(r)], here.relay_to)

    def c_over(r):
        return copies.make(("c_over", r), crelay.at[CACHE_MINUS.index(r)], cache.at[3, part_rows(r)], here.pass_to)

    def c_near(r):
        return copies.make(("c_near", r), cache.at[1, part_rows(r)], cache.at[2 * (1 - c), part_rows(r)], here.partner)

    def c_far(r):
        return copies.make(("c_far", r), cache.at[4 - c, part_rows(r)], cache.at[2 * c, part_rows(r)], here.partner)

    def hand_on(r):
        to_right(r).wait_recv()
        go(on_right(r))
        to_left(r).wait_recv()
        go(on_left(r))

    def make_part(r):
        on_right(r).wait_recv()
        on_left(r).wait_recv()
        wide = hid[r * TILE:(r + 1) * TILE, :].astype(F32)
        mean_square = jnp.sum(wide * wide, axis=1, keepdims=True) / D
        normed = (wide * lax.rsqrt(mean_square + EPSILON) * gain_ref[...]).astype(BF16)
        made = jnp.dot(normed, wall[:, :, :, :, WIDTH:].reshape(D, CACHE), preferred_element_type=F32).astype(BF16)
        cache[4, r * TILE:(r + 1) * TILE, :] = made
        asked = jnp.dot(normed, wall[:, :, :, :, :WIDTH].reshape(D, WIDTH), preferred_element_type=F32).astype(BF16)
        queries[r * TILE:(r + 1) * TILE, :] = asked
        go(c_forth(r))
        if r in CACHE_MINUS:
            go(c_back(r))

    def c_arrive(r):
        c_forth(r).wait_recv()
        go(c_near(r))
        if r in CACHE_PLUS:
            go(c_again(r))
        else:
            c_back(r).wait_recv()
            go(c_over(r))

    def complete(r):
        (c_again if r in CACHE_PLUS else c_over)(r).wait_recv()
        go(c_far(r))

    for r in (0, 1):
        go(to_right(r))
        go(to_left(r))
    sunk(4, 0, last=True)
    risen(0, 0)
    hand_on(0)
    go(to_right(2))
    go(to_left(2))
    sunk(4, 1, last=True)
    risen(0, 1)
    hand_on(1)
    go(to_right(3))
    go(to_left(3))
    risen(1, 0, last=True)
    risen(1, 1, last=True)
    for steps in range(-2, 6):
        for part in (0, 1):
            share(steps, part).wait_recv()
    make_part(0)
    hand_on(2)
    make_part(1)
    c_arrive(0)
    hand_on(3)
    make_part(2)
    c_arrive(1)
    complete(0)
    make_part(3)
    c_arrive(2)
    complete(1)

    def head_cols(h):
        return pl.ds(pl.multiple_of(h * HEAD_DIM, HEAD_DIM), HEAD_DIM)

    def step(h, slot, limit, state, past=None):
        g = h // 3
        return flash_step(
            queries[:, head_cols(h)],
            cache[slot, :, head_cols(g)],
            cache[slot, :, head_cols(g + 2)],
            limit, state, past,
        )

    def own_keys(h, carry):
        put_state(refs, h, step(h, 4, limits[0], None, "own"))
        return carry

    lax.fori_loop(0, HEADS, own_keys, 0)
    c_arrive(3)
    complete(2)
    for r in range(PARTS):
        c_near(r).wait_recv()

    def near_keys(h, carry):
        state = step(h, 1, limits[2], get_state(refs, h))
        put_state(refs, h, step(h, 2 * c, near_limit, state))
        return carry

    lax.fori_loop(0, HEADS, near_keys, 0)
    complete(3)
    for r in range(PARTS):
        c_far(r).wait_recv()

    def far_keys(h, carry):
        state = step(h, 3, limits[4], get_state(refs, h))
        state = step(h, 2 * (1 - c), far_limit, state)
        out_ref[:, head_cols(h)] = (state[2] / state[1]).astype(BF16)
        return carry

    lax.fori_loop(0, HEADS, far_keys, 0)
    for copy in started:
        copy.wait_send()
    assert len(copies.made) == N_COPIES, len(copies.made)


N_COPIES = 61 + 3 + 10 + 4 + 16 + 34


def layer(doc, tail, q, res, gain, k, v, wo, wq, wc):
    any_spec = pl.BlockSpec(memory_space=pl.ANY)
    vmem = pl.BlockSpec(memory_space=pltpu.VMEM)
    smem = pl.BlockSpec(memory_space=pltpu.SMEM)
    return pl.pallas_call(
        layer_kernel,
        out_shape=(jax.ShapeDtypeStruct((ROWS, WIDTH), BF16),) * 2,
        in_specs=[smem, smem, vmem, vmem, vmem] + [any_spec] * 5,
        out_specs=(vmem, vmem),
        scratch_shapes=[
            pltpu.VMEM((SLOTS, HEADS, 2, ROWS, HEAD_DIM), BF16),
            pltpu.VMEM((len(MINUS), 2, ROWS, HEAD_DIM), BF16),
            pltpu.VMEM((ROWS, D), BF16),
            pltpu.VMEM((D, WIDTH), BF16),
            pltpu.VMEM((2, HALF // 2, WIDTH), BF16),
            pltpu.VMEM((ROWS, WIDTH), F32),
            *STATE,
            pltpu.VMEM((ROWS, D), BF16),
            pltpu.VMEM((GROUPS, 4, 2, SHARD, COLS), BF16),
            pltpu.VMEM((SLOTS, ROWS, CACHE), BF16),
            pltpu.VMEM((len(CACHE_MINUS), TILE, CACHE), BF16),
            pltpu.VMEM((ROWS, WIDTH), BF16),
            pltpu.SemaphoreType.DMA((2 * HEADS + 3,)),
            pltpu.SemaphoreType.DMA((N_COPIES,)),
            pltpu.SemaphoreType.DMA((N_COPIES,)),
        ],
        compiler_params=pltpu.CompilerParams(
            collective_id=0, has_side_effects=True, vmem_limit_bytes=60 * 1024 * 1024
        ),
        name="layer",
    )(doc, tail, q, res, gain, k, v, wo, wq, wc)


def local(
    residual, q_self, k_self, v_self, w_out, norm_gain, w_query, w_cache, block_doc, tail_len
):
    return layer(
        block_doc, tail_len, q_self, residual, norm_gain.reshape(1, D),
        k_self, v_self, w_out, w_query, w_cache,
    )


def solution(mesh):
    in_specs = (
        P("seq", "head"),
        P("seq", "head"),
        P("seq", "head"),
        P("seq", "head"),
        P("head", None),
        P(),
        P("seq", "head"),
        P("seq", "head"),
        P(),
        P(),
    )
    out_specs = (P("seq", "head"), P("seq", "head"))
    return jax.shard_map(local, mesh=mesh, in_specs=in_specs, out_specs=out_specs, check_vma=False)
```

time: 200 us -> 174 us (0.87)
  Pallas kernels: 192 us -> 167 us
    pallas_call x2 -> x1, Pallas kernels: 192 us -> 167 us  [layer(): pl.pallas_call(layer_kernel, out_shape=(jax.ShapeDtypeStruct((ROWS, WIDTH...]
    unnamed x4 -> x2, local copies, waits for them, and re-layouts: 2.95 us -> 4.13 us
where the time goes in v3:
time: 174 us; the launch traced here: 172 us
  Pallas kernels  167 us (96%)
  local copies, waits for them, and re-layouts  4.13 us (2%)
    pallas_call x1, Pallas kernels, layer(): pl.pallas_call(layer_kernel, out_shape=(jax.ShapeDtypeStruct((ROWS, WIDTH...  167 us
    unnamed x2, local copies, waits for them, and re-layouts  4.13 us

profile of v3, /device:TPU:9, one launch (start us, length us, event | category | flops | bytes accessed | tf_op | source)
XLA Modules:
  0.0 171.5 jit_solution(11967462395841015398)
XLA Ops:
  0.6 166.8 %layer.1 = (bf16[512,768]{1,0:T(8,128)(2,1)}, bf16[512,768]{1,0:T(8,128)(2,1)}) custom-call(s32[64]{0:T(128)} %doc_ref.1, s32[64]{0:T(128)} %tail_ref.1, bf16[512,768]{1,0:T(8,128)(2,1)} %q_ref.1, bf16[512,768]{1,0:T(8,128)(2,1)} %res_ref.1, f32[1,3072]{1,0:T(1,128)} %bitcast.1, bf16[512,768]{1,0:T(8,128)(2,1)} %k_hbm.1, bf16[512,768]{1,0:T(8,128)(2,1)} %v_hbm.1, ...), custom_call_target="tpu_custom_call" | custom-call | tf_op jit(solution)/shard_map/layer/pallas_call | solution.py:621
  167.4 2.1 %copy.14 = bf16[512,768]{1,0:T(8,128)(2,1)} copy(bf16[512,768]{1,0:T(8,128)(2,1)} %get-tuple-element.4) | data formatting | bytes 1572864
  169.5 2.1 %copy.15 = bf16[512,768]{1,0:T(8,128)(2,1)} copy(bf16[512,768]{1,0:T(8,128)(2,1)} %get-tuple-element.5) | data formatting | bytes 1572864

commit v4 on v3

--- a/solution.py
+++ b/solution.py
@@ -83,6 +83,7 @@
         self.partner = (i + 1 - 2 * c, x)
         self.right = (i, (x + 1) % 4)
         self.left = (i, (x + 3) % 4)
+        self.across = (i, (x + 2) % 4)
         self.y_up, self.y_down = (at(z, up, c), x), (at(z, down, c), x)
         self.y_far = (at(z, (y + 2) % 4, c), x)
         self.z_up, self.z_down = (at(z + 1, y, c), x), (at(z - 1, y, c), x)
@@ -154,8 +155,8 @@
 def layer_kernel(
     doc_ref, tail_ref, q_ref, res_ref, gain_ref, k_hbm, v_hbm, wo_hbm, wq_hbm, wc_hbm,
     hidden_ref, out_ref,
-    kv, relay, ctx, woc, wrelay, acc, peak_ref, total_ref, blended_ref,
-    hid, wall, cache, crelay, queries, local_sem, send_sem, recv_sem,
+    kv, relay, ctx, woc, acc, peak_ref, total_ref, blended_ref,
+    hid, wall, cache, crelay, queries, local_sem, send_sem, recv_sem, clear_sem,
 ):
     refs = (peak_ref, total_ref, blended_ref)
     here = Place()
@@ -186,7 +187,7 @@
 
     greet([
         here.next_chip, here.prev_chip, here.relay_to, here.relay_from, here.pass_to, here.pass_from,
-        here.partner, here.right, here.left, here.y_up, here.y_down, here.y_far, here.y_far, here.z_up, here.z_down,
+        here.partner, here.right, here.left, here.across, here.across, here.y_up, here.y_down, here.y_far, here.y_far, here.z_up, here.z_down,
     ])
 
     def go(copy):
@@ -233,16 +234,10 @@
     def w_cols(block):
         return pl.ds(pl.multiple_of(block * WIDTH, WIDTH), WIDTH)
 
-    quarter = HALF // 2
     c_half = pl.ds(pl.multiple_of(c * HALF, HALF), HALF)
-    c_one = pl.ds(pl.multiple_of(c * HALF, 64), quarter)
-    c_two = pl.ds(pl.multiple_of(c * HALF + quarter, 64), quarter)
     w_right = copies.make("wr", wo_hbm.at[c_half, w_cols(right_x)], woc.at[w_rows(x, 0, HALF)], here.right)
     w_left = copies.make("wl", wo_hbm.at[c_half, w_cols(left_x)], woc.at[w_rows(x, 0, HALF)], here.left)
-    w_far_r = copies.make("wfr", wo_hbm.at[c_one, w_cols(far_x)], wrelay.at[0], here.right)
-    w_far_l = copies.make("wfl", wo_hbm.at[c_two, w_cols(far_x)], wrelay.at[1], here.left)
-    w_on_r = copies.make("wor", wrelay.at[0], woc.at[w_rows(left_x, 0, quarter)], here.right)
-    w_on_l = copies.make("wol", wrelay.at[1], woc.at[w_rows(right_x, quarter, quarter)], here.left)
+    w_far = copies.make("wf", wo_hbm.at[c_half, w_cols(far_x)], woc.at[w_rows(x, 0, HALF)], here.across)
 
     def w_twin(name, block):
         rows = w_rows(block, 0, HALF)
@@ -255,31 +250,27 @@
     def ctx_cols(block, h):
         return pl.ds(pl.multiple_of(block * WIDTH + h * HEAD_DIM, HEAD_DIM), HEAD_DIM)
 
-    upper, lower = pl.ds(0, ROWS // 2), pl.ds(ROWS // 2, ROWS // 2)
-
     def ctx_right(h):
         return copies.make(("cr", h), ctx.at[:, ctx_cols(x, h)], ctx.at[:, ctx_cols(x, h)], here.right)
 
     def ctx_left(h):
         return copies.make(("cl", h), ctx.at[:, ctx_cols(x, h)], ctx.at[:, ctx_cols(x, h)], here.left)
 
-    def ctx_on_right(h):
-        part = ctx.at[upper, ctx_cols(left_x, h)]
-        return copies.make(("cor", h), part, part, here.right)
-
-    def ctx_on_left(h):
-        part = ctx.at[lower, ctx_cols(right_x, h)]
-        return copies.make(("col", h), part, part, here.left)
+    def ctx_across(h):
+        return copies.make(("ca", h), ctx.at[:, ctx_cols(x, h)], ctx.at[:, ctx_cols(x, h)], here.across)
 
     limits = key_limits(doc_ref, tail_ref, i)
 
     near_limit = jnp.where(c == 0, limits[1], limits[3])
     far_limit = jnp.where(c == 0, limits[3], limits[1])
 
+    def own_keys(h):
+        q = q_ref[:, h * HEAD_DIM:(h + 1) * HEAD_DIM]
+        put_state(refs, h, flash_step(q, kv[4, h, 0], kv[4, h, 1], limits[0], None, "own"))
+
     def first_keys(h):
         q = q_ref[:, h * HEAD_DIM:(h + 1) * HEAD_DIM]
-        state = flash_step(q, kv[4, h, 0], kv[4, h, 1], limits[0], None, "own")
-        state = flash_step(q, kv[1, h, 0], kv[1, h, 1], limits[2], state)
+        state = flash_step(q, kv[1, h, 0], kv[1, h, 1], limits[2], get_state(refs, h))
         near = 2 * c
         state = flash_step(q, kv[near, h, 0], kv[near, h, 1], near_limit, state)
         put_state(refs, h, state)
@@ -293,12 +284,12 @@
         ctx[:, ctx_cols(x, h)] = (state[2] / state[1]).astype(BF16)
         go(ctx_right(h))
         go(ctx_left(h))
-
-    def pass_context(h):
+        go(ctx_across(h))
+
+    def take_context(h):
         ctx_right(h).wait_recv()
-        go(ctx_on_right(h))
         ctx_left(h).wait_recv()
-        go(ctx_on_left(h))
+        ctx_across(h).wait_recv()
 
     def sunk(n, part, last=False):
         sink(n, part).wait_recv()
@@ -314,31 +305,36 @@
 
     for copy in shard_loads:
         copy.wait()
-    go(shard_up)
-    go(shard_down)
-    go(shard_far)
-    for h in (0, 1, 2):
+    shards = (shard_up, shard_down, shard_far)
+    for copy in shards:
+        copy.start()
+    go(w_right)
+    go(w_left)
+    go(w_far)
+    for copy in local[0] + local[1]:
+        copy.wait()
+    own_keys(0)
+    own_keys(1)
+    for h in (2, 3, 4, 5):
         for copy in local[h]:
             copy.wait()
+    own_keys(2)
+    for copy in shards:
+        copy.wait_send()
+    pl.semaphore_signal(clear_sem, inc=1, device_id=here.z_down, device_id_type=MESH)
+    pl.semaphore_wait(clear_sem, 1)
     go(forth(0))
     go(back(1))
-    go(w_right)
-    go(w_left)
-    go(w_far_r)
-    go(w_far_l)
     go(forth(1))
     go(back(2))
-    for h in (3, 4, 5):
-        for copy in local[h]:
-            copy.wait()
     own_w.wait()
-
-    shard_up.wait_recv()
-    shard_down.wait_recv()
-    shard_far.wait_recv()
+    for copy in shards:
+        copy.wait_recv()
     for part in (0, 1):
         go(sink(0, part))
         go(share(0, part))
+    for h in (3, 4, 5):
+        own_keys(h)
     back(1).wait_recv()
     go(over(1))
     go(back(4))
@@ -362,10 +358,8 @@
     go(w_twin_l)
     w_left.wait_recv()
     go(w_twin_r)
-    w_far_r.wait_recv()
-    go(w_on_r)
-    w_far_l.wait_recv()
-    go(w_on_l)
+    w_far.wait_recv()
+    go(w_twin_f)
     over(1).wait_recv()
     go(twin_far(1))
     again(0).wait_recv()
@@ -383,17 +377,12 @@
     go(forth(5))
     go(twin_near(3))
     sunk(1, 1)
-    w_on_r.wait_recv()
-    w_on_l.wait_recv()
-    go(w_twin_f)
     twin_near(3).wait_recv()
     first_keys(3)
     over(2).wait_recv()
     go(twin_far(2))
     forth(2).wait_recv()
     go(twin_near(2))
-    pass_context(1)
-    pass_context(0)
     twin_near(2).wait_recv()
     first_keys(2)
     twin_far(2).wait_recv()
@@ -406,7 +395,6 @@
     sunk(2, 1)
     twin_far(3).wait_recv()
     last_keys(3)
-    pass_context(2)
     over(4).wait_recv()
     go(twin_far(4))
     forth(4).wait_recv()
@@ -418,7 +406,6 @@
     twin_far(4).wait_recv()
     last_keys(4)
     sunk(3, 0)
-    pass_context(3)
     over(5).wait_recv()
     go(twin_far(5))
     forth(5).wait_recv()
@@ -428,12 +415,10 @@
     twin_far(5).wait_recv()
     last_keys(5)
     sunk(3, 1)
-    pass_context(4)
     for copy in (w_twin_l, w_twin_r, w_twin_f):
         copy.wait_recv()
     for h in range(4):
-        ctx_on_right(h).wait_recv()
-        ctx_on_left(h).wait_recv()
+        take_context(h)
 
     def project(first, count, seed, store):
         def tile(t, carry):
@@ -461,10 +446,8 @@
         hid[rows, cols(x)] = tile
 
     project(0, 4 * HEAD_DIM, lambda rows: jnp.zeros((TILE, WIDTH), F32), keep)
-    pass_context(5)
-    for h in (4, 5):
-        ctx_on_right(h).wait_recv()
-        ctx_on_left(h).wait_recv()
+    take_context(4)
+    take_context(5)
     project(4 * HEAD_DIM, 2 * HEAD_DIM, lambda rows: acc[rows, :], finish)
 
     def part_rows(r):
@@ -478,13 +461,9 @@
         part = hid.at[part_rows(r), cols(x)]
         return copies.make(("l", r), part, part, here.left)
 
-    def on_right(r):
-        part = hid.at[pl.ds(r * TILE, TILE // 2), cols(left_x)]
-        return copies.make(("or", r), part, part, here.right)
-
-    def on_left(r):
-        part = hid.at[pl.ds(r * TILE + TILE // 2, TILE // 2), cols(right_x)]
-        return copies.make(("ol", r), part, part, here.left)
+    def to_far(r):
+        part = hid.at[part_rows(r), cols(x)]
+        return copies.make(("a", r), part, part, here.across)
 
     def c_forth(r):
         return copies.make(("c_forth", r), cache.at[4, part_rows(r)], cache.at[1, part_rows(r)], here.next_chip)
@@ -504,15 +483,10 @@
     def c_far(r):
         return copies.make(("c_far", r), cache.at[4 - c, part_rows(r)], cache.at[2 * c, part_rows(r)], here.partner)
 
-    def hand_on(r):
+    def make_part(r):
         to_right(r).wait_recv()
-        go(on_right(r))
         to_left(r).wait_recv()
-        go(on_left(r))
-
-    def make_part(r):
-        on_right(r).wait_recv()
-        on_left(r).wait_recv()
+        to_far(r).wait_recv()
         wide = hid[r * TILE:(r + 1) * TILE, :].astype(F32)
         mean_square = jnp.sum(wide * wide, axis=1, keepdims=True) / D
         normed = (wide * lax.rsqrt(mean_square + EPSILON) * gain_ref[...]).astype(BF16)
@@ -537,29 +511,22 @@
         (c_again if r in CACHE_PLUS else c_over)(r).wait_recv()
         go(c_far(r))
 
-    for r in (0, 1):
+    for r in range(PARTS):
         go(to_right(r))
         go(to_left(r))
+        go(to_far(r))
     sunk(4, 0, last=True)
     risen(0, 0)
-    hand_on(0)
-    go(to_right(2))
-    go(to_left(2))
     sunk(4, 1, last=True)
     risen(0, 1)
-    hand_on(1)
-    go(to_right(3))
-    go(to_left(3))
     risen(1, 0, last=True)
     risen(1, 1, last=True)
     for steps in range(-2, 6):
         for part in (0, 1):
             share(steps, part).wait_recv()
     make_part(0)
-    hand_on(2)
     make_part(1)
     c_arrive(0)
-    hand_on(3)
     make_part(2)
     c_arrive(1)
     complete(0)
@@ -579,11 +546,11 @@
             limit, state, past,
         )
 
-    def own_keys(h, carry):
+    def c_own_keys(h, carry):
         put_state(refs, h, step(h, 4, limits[0], None, "own"))
         return carry
 
-    lax.fori_loop(0, HEADS, own_keys, 0)
+    lax.fori_loop(0, HEADS, c_own_keys, 0)
     c_arrive(3)
     complete(2)
     for r in range(PARTS):
@@ -611,7 +578,7 @@
     assert len(copies.made) == N_COPIES, len(copies.made)
 
 
-N_COPIES = 61 + 3 + 10 + 4 + 16 + 34
+N_COPIES = 28 + 6 + 18 + 3 + 10 + 4 + 16 + 12 + 18
 
 
 def layer(doc, tail, q, res, gain, k, v, wo, wq, wc):
@@ -628,7 +595,6 @@
             pltpu.VMEM((len(MINUS), 2, ROWS, HEAD_DIM), BF16),
             pltpu.VMEM((ROWS, D), BF16),
             pltpu.VMEM((D, WIDTH), BF16),
-            pltpu.VMEM((2, HALF // 2, WIDTH), BF16),
             pltpu.VMEM((ROWS, WIDTH), F32),
             *STATE,
             pltpu.VMEM((ROWS, D), BF16),
@@ -639,6 +605,7 @@
             pltpu.SemaphoreType.DMA((2 * HEADS + 3,)),
             pltpu.SemaphoreType.DMA((N_COPIES,)),
             pltpu.SemaphoreType.DMA((N_COPIES,)),
+            pltpu.SemaphoreType.REGULAR,
         ],
         compiler_params=pltpu.CompilerParams(
             collective_id=0, has_side_effects=True, vmem_limit_bytes=60 * 1024 * 1024

time: 174 us -> 152 us (0.87)
  Pallas kernels: 167 us -> 145 us
    pallas_call x1, Pallas kernels: 167 us -> 145 us  [layer(): pl.pallas_call(layer_kernel, out_shape=(jax.ShapeDtypeStruct((ROWS, WIDTH...]
where the time goes in v4:
time: 152 us; the launch traced here: 150 us
  Pallas kernels  145 us (95%)
  local copies, waits for them, and re-layouts  4.13 us (3%)
    pallas_call x1, Pallas kernels, layer(): pl.pallas_call(layer_kernel, out_shape=(jax.ShapeDtypeStruct((ROWS, WIDTH...  145 us
    unnamed x2, local copies, waits for them, and re-layouts  4.13 us

profile of v4, /device:TPU:9, one launch (start us, length us, event | category | flops | bytes accessed | tf_op | source)
XLA Modules:
  0.0 150.1 jit_solution(11718342773274243164)
XLA Ops:
  0.6 145.3 %layer.1 = (bf16[512,768]{1,0:T(8,128)(2,1)}, bf16[512,768]{1,0:T(8,128)(2,1)}) custom-call(s32[64]{0:T(128)} %doc_ref.1, s32[64]{0:T(128)} %tail_ref.1, bf16[512,768]{1,0:T(8,128)(2,1)} %q_ref.1, bf16[512,768]{1,0:T(8,128)(2,1)} %res_ref.1, f32[1,3072]{1,0:T(1,128)} %bitcast.1, bf16[512,768]{1,0:T(8,128)(2,1)} %k_hbm.1, bf16[512,768]{1,0:T(8,128)(2,1)} %v_hbm.1, ...), custom_call_target="tpu_custom_call" | custom-call | tf_op jit(solution)/shard_map/layer/pallas_call | solution.py:588
  146.0 2.1 %copy.14 = bf16[512,768]{1,0:T(8,128)(2,1)} copy(bf16[512,768]{1,0:T(8,128)(2,1)} %get-tuple-element.4) | data formatting | bytes 1572864
  148.0 2.1 %copy.15 = bf16[512,768]{1,0:T(8,128)(2,1)} copy(bf16[512,768]{1,0:T(8,128)(2,1)} %get-tuple-element.5) | data formatting | bytes 1572864

commit v5 on v4

--- a/solution.py
+++ b/solution.py
@@ -343,34 +343,32 @@
     go(forth(3))
     go(twin_near(0))
     twin_near(0).wait_recv()
+    sunk(0, 0)
     first_keys(0)
-    sunk(0, 0)
+    forth(1).wait_recv()
+    go(forth(2))
+    go(twin_near(1))
+    sunk(0, 1)
+    twin_near(1).wait_recv()
+    first_keys(1)
+    over(1).wait_recv()
+    go(twin_far(1))
+    again(0).wait_recv()
+    go(twin_far(0))
     back(2).wait_recv()
     go(over(2))
     go(back(5))
-    forth(1).wait_recv()
-    go(forth(2))
-    go(twin_near(1))
-    twin_near(1).wait_recv()
-    first_keys(1)
-    sunk(0, 1)
+    twin_far(1).wait_recv()
+    last_keys(1)
+    sunk(1, 0)
+    twin_far(0).wait_recv()
+    last_keys(0)
     w_right.wait_recv()
     go(w_twin_l)
     w_left.wait_recv()
     go(w_twin_r)
     w_far.wait_recv()
     go(w_twin_f)
-    over(1).wait_recv()
-    go(twin_far(1))
-    again(0).wait_recv()
-    go(twin_far(0))
-    twin_far(1).wait_recv()
-    last_keys(1)
-    twin_far(0).wait_recv()
-    last_keys(0)
-    sunk(1, 0)
-    back(4).wait_recv()
-    go(over(4))
     forth(3).wait_recv()
     go(again(3))
     go(forth(4))
@@ -379,39 +377,41 @@
     sunk(1, 1)
     twin_near(3).wait_recv()
     first_keys(3)
+    forth(2).wait_recv()
+    go(twin_near(2))
+    back(4).wait_recv()
+    go(over(4))
+    sunk(2, 0)
+    twin_near(2).wait_recv()
+    first_keys(2)
     over(2).wait_recv()
     go(twin_far(2))
-    forth(2).wait_recv()
-    go(twin_near(2))
-    twin_near(2).wait_recv()
-    first_keys(2)
     twin_far(2).wait_recv()
     last_keys(2)
     back(5).wait_recv()
     go(over(5))
-    sunk(2, 0)
     again(3).wait_recv()
     go(twin_far(3))
+    for part in (0, 1):
+        go(rise(0, part))
     sunk(2, 1)
     twin_far(3).wait_recv()
     last_keys(3)
+    forth(4).wait_recv()
+    go(twin_near(4))
+    twin_near(4).wait_recv()
+    first_keys(4)
     over(4).wait_recv()
     go(twin_far(4))
-    forth(4).wait_recv()
-    go(twin_near(4))
-    for part in (0, 1):
-        go(rise(0, part))
-    twin_near(4).wait_recv()
-    first_keys(4)
+    sunk(3, 0)
     twin_far(4).wait_recv()
     last_keys(4)
-    sunk(3, 0)
-    over(5).wait_recv()
-    go(twin_far(5))
     forth(5).wait_recv()
     go(twin_near(5))
     twin_near(5).wait_recv()
     first_keys(5)
+    over(5).wait_recv()
+    go(twin_far(5))
     twin_far(5).wait_recv()
     last_keys(5)
     sunk(3, 1)
@@ -461,9 +461,13 @@
         part = hid.at[part_rows(r), cols(x)]
         return copies.make(("l", r), part, part, here.left)
 
-    def to_far(r):
-        part = hid.at[part_rows(r), cols(x)]
-        return copies.make(("a", r), part, part, here.across)
+    def on_right(r):
+        part = hid.at[pl.ds(r * TILE, TILE // 2), cols(left_x)]
+        return copies.make(("or", r), part, part, here.right)
+
+    def on_left(r):
+        part = hid.at[pl.ds(r * TILE + TILE // 2, TILE // 2), cols(right_x)]
+        return copies.make(("ol", r), part, part, here.left)
 
     def c_forth(r):
         return copies.make(("c_forth", r), cache.at[4, part_rows(r)], cache.at[1, part_rows(r)], here.next_chip)
@@ -483,10 +487,19 @@
     def c_far(r):
         return copies.make(("c_far", r), cache.at[4 - c, part_rows(r)], cache.at[2 * c, part_rows(r)], here.partner)
 
+    def hand_on(r):
+        to_right(r).wait_recv()
+        go(on_right(r))
+        to_left(r).wait_recv()
+        go(on_left(r))
+
+    def send_part(r):
+        go(to_right(r))
+        go(to_left(r))
+
     def make_part(r):
-        to_right(r).wait_recv()
-        to_left(r).wait_recv()
-        to_far(r).wait_recv()
+        on_right(r).wait_recv()
+        on_left(r).wait_recv()
         wide = hid[r * TILE:(r + 1) * TILE, :].astype(F32)
         mean_square = jnp.sum(wide * wide, axis=1, keepdims=True) / D
         normed = (wide * lax.rsqrt(mean_square + EPSILON) * gain_ref[...]).astype(BF16)
@@ -511,28 +524,31 @@
         (c_again if r in CACHE_PLUS else c_over)(r).wait_recv()
         go(c_far(r))
 
-    for r in range(PARTS):
-        go(to_right(r))
-        go(to_left(r))
-        go(to_far(r))
+    send_part(0)
+    send_part(1)
+    risen(0, 0)
+    risen(0, 1)
     sunk(4, 0, last=True)
-    risen(0, 0)
+    hand_on(0)
+    send_part(2)
     sunk(4, 1, last=True)
-    risen(0, 1)
+    hand_on(1)
+    send_part(3)
     risen(1, 0, last=True)
     risen(1, 1, last=True)
     for steps in range(-2, 6):
         for part in (0, 1):
             share(steps, part).wait_recv()
     make_part(0)
+    hand_on(2)
     make_part(1)
     c_arrive(0)
+    hand_on(3)
     make_part(2)
     c_arrive(1)
     complete(0)
     make_part(3)
     c_arrive(2)
-    complete(1)
 
     def head_cols(h):
         return pl.ds(pl.multiple_of(h * HEAD_DIM, HEAD_DIM), HEAD_DIM)
@@ -552,6 +568,7 @@
 
     lax.fori_loop(0, HEADS, c_own_keys, 0)
     c_arrive(3)
+    complete(1)
     complete(2)
     for r in range(PARTS):
         c_near(r).wait_recv()
@@ -578,7 +595,7 @@
     assert len(copies.made) == N_COPIES, len(copies.made)
 
 
-N_COPIES = 28 + 6 + 18 + 3 + 10 + 4 + 16 + 12 + 18
+N_COPIES = 28 + 6 + 18 + 3 + 10 + 4 + 16 + 16 + 18
 
 
 def layer(doc, tail, q, res, gain, k, v, wo, wq, wc):

time: 152 us -> 144 us (0.947)
  Pallas kernels: 145 us -> 138 us
    pallas_call x1, Pallas kernels: 145 us -> 138 us  [layer(): pl.pallas_call(layer_kernel, out_shape=(jax.ShapeDtypeStruct((ROWS, WIDTH...]
where the time goes in v5:
time: 144 us; the launch traced here: 143 us
  Pallas kernels  138 us (96%)
  local copies, waits for them, and re-layouts  4.13 us (3%)
    pallas_call x1, Pallas kernels, layer(): pl.pallas_call(layer_kernel, out_shape=(jax.ShapeDtypeStruct((ROWS, WIDTH...  138 us
    unnamed x2, local copies, waits for them, and re-layouts  4.13 us

profile of v5, /device:TPU:9, one launch (start us, length us, event | category | flops | bytes accessed | tf_op | source)
XLA Modules:
  0.0 142.8 jit_solution(14908594979382760732)
XLA Ops:
  0.6 138.0 %layer.1 = (bf16[512,768]{1,0:T(8,128)(2,1)}, bf16[512,768]{1,0:T(8,128)(2,1)}) custom-call(s32[64]{0:T(128)} %doc_ref.1, s32[64]{0:T(128)} %tail_ref.1, bf16[512,768]{1,0:T(8,128)(2,1)} %q_ref.1, bf16[512,768]{1,0:T(8,128)(2,1)} %res_ref.1, f32[1,3072]{1,0:T(1,128)} %bitcast.1, bf16[512,768]{1,0:T(8,128)(2,1)} %k_hbm.1, bf16[512,768]{1,0:T(8,128)(2,1)} %v_hbm.1, ...), custom_call_target="tpu_custom_call" | custom-call | tf_op jit(solution)/shard_map/layer/pallas_call | solution.py:605
  138.6 2.1 %copy.14 = bf16[512,768]{1,0:T(8,128)(2,1)} copy(bf16[512,768]{1,0:T(8,128)(2,1)} %get-tuple-element.4) | data formatting | bytes 1572864
  140.7 2.1 %copy.15 = bf16[512,768]{1,0:T(8,128)(2,1)} copy(bf16[512,768]{1,0:T(8,128)(2,1)} %get-tuple-element.5) | data formatting | bytes 1572864

commit v6 on v5

--- a/solution.py
+++ b/solution.py
@@ -110,19 +110,19 @@
     return limits
 
 
-def flash_step(q, keys, values, limit, state, past=None):
-    rows = q.shape[0]
-    lane = lax.broadcasted_iota(jnp.int32, (1, ROWS), 1)
+def flash_step(q, keys, values, limit, state, past=None, first=0):
+    rows, count = q.shape[0], keys.shape[0]
+    lane = lax.broadcasted_iota(jnp.int32, (1, count), 1)
     s = lax.dot_general(q, keys, (((1,), (1,)), ((), ())), preferred_element_type=F32)
     s = jnp.minimum(s, jnp.where(lane < limit, LARGE, MASKED))
     if past is not None:
-        query_at = lax.broadcasted_iota(jnp.int32, (rows, ROWS), 0)
-        key_at = lax.broadcasted_iota(jnp.int32, (rows, ROWS), 1)
+        query_at = first + lax.broadcasted_iota(jnp.int32, (rows, count), 0)
+        key_at = lax.broadcasted_iota(jnp.int32, (rows, count), 1)
         s = jnp.where(key_at <= query_at if past == "own" else key_at > query_at, s, MASKED)
     peak = jnp.max(s, axis=1, keepdims=True)
     if state is not None:
         peak = jnp.maximum(peak, state[0])
-    spread = peak if peak.shape[1] == 1 else jnp.concatenate([peak] * (ROWS // HEAD_DIM), axis=1)
+    spread = peak if peak.shape[1] == 1 else jnp.concatenate([peak] * (count // HEAD_DIM), axis=1)
     weights = jnp.exp2((s - spread) * EXP2_SCALE)
     total = jnp.sum(weights, axis=1, keepdims=True)
     blended = jnp.dot(weights.astype(BF16), values, preferred_element_type=F32)
@@ -133,11 +133,11 @@
     return peak, total, blended
 
 
-def put_state(refs, h, state):
+def put_state(refs, h, state, rows=slice(0, ROWS)):
     peak_ref, total_ref, blended_ref = refs
-    peak_ref[h] = jnp.broadcast_to(state[0], (ROWS, HEAD_DIM))
-    total_ref[h] = jnp.broadcast_to(state[1], (ROWS, HEAD_DIM))
-    blended_ref[h] = state[2]
+    peak_ref[h, rows] = jnp.broadcast_to(state[0], state[2].shape)
+    total_ref[h, rows] = jnp.broadcast_to(state[1], state[2].shape)
+    blended_ref[h, rows] = state[2]
 
 
 def get_state(refs, h):
@@ -153,8 +153,8 @@
 
 
 def layer_kernel(
-    doc_ref, tail_ref, q_ref, res_ref, gain_ref, k_hbm, v_hbm, wo_hbm, wq_hbm, wc_hbm,
-    hidden_ref, out_ref,
+    doc_ref, tail_ref, gain_ref, q_hbm, res_hbm, k_hbm, v_hbm, wo_hbm, wq_hbm, wc_hbm,
+    hidden_hbm, out_hbm, q_ref, res_ref, out_ref,
     kv, relay, ctx, woc, acc, peak_ref, total_ref, blended_ref,
     hid, wall, cache, crelay, queries, local_sem, send_sem, recv_sem, clear_sem,
 ):
@@ -165,6 +165,8 @@
     started = []
     right_x, left_x, far_x = (x + 1) % 4, (x + 3) % 4, (x + 2) % 4
 
+    load_q = pltpu.make_async_copy(q_hbm, q_ref, local_sem.at[2 * HEADS + 3])
+    load_q.start()
     local = []
     for h in range(HEADS):
         cols = pl.ds(h * HEAD_DIM, HEAD_DIM)
@@ -184,6 +186,8 @@
     )
     for copy in shard_loads:
         copy.start()
+    load_res = pltpu.make_async_copy(res_hbm, res_ref, local_sem.at[2 * HEADS + 4])
+    load_res.start()
 
     greet([
         here.next_chip, here.prev_chip, here.relay_to, here.relay_from, here.pass_to, here.pass_from,
@@ -313,6 +317,7 @@
     go(w_far)
     for copy in local[0] + local[1]:
         copy.wait()
+    load_q.wait()
     own_keys(0)
     own_keys(1)
     for h in (2, 3, 4, 5):
@@ -420,19 +425,15 @@
     for h in range(4):
         take_context(h)
 
-    def project(first, count, seed, store):
-        def tile(t, carry):
-            rows = pl.ds(pl.multiple_of(t * TILE, TILE), TILE)
-            total = seed(rows)
-            for block in range(4):
-                at = block * WIDTH + first
-                total = total + jnp.dot(
-                    ctx[rows, at:at + count], woc[at:at + count, :], preferred_element_type=F32
-                )
-            store(rows, total)
-            return carry
-
-        lax.fori_loop(0, ROWS // TILE, tile, 0)
+    def project_tile(t, first, count, seed, store):
+        rows = pl.ds(pl.multiple_of(t * TILE, TILE), TILE)
+        total = seed(rows)
+        for block in range(4):
+            at = block * WIDTH + first
+            total = total + jnp.dot(
+                ctx[rows, at:at + count], woc[at:at + count, :], preferred_element_type=F32
+            )
+        store(rows, total)
 
     def keep(rows, total):
         acc[rows, :] = total
@@ -442,13 +443,19 @@
 
     def finish(rows, total):
         tile = (res_ref[rows, :].astype(F32) + total).astype(BF16)
-        hidden_ref[rows, :] = tile
         hid[rows, cols(x)] = tile
 
-    project(0, 4 * HEAD_DIM, lambda rows: jnp.zeros((TILE, WIDTH), F32), keep)
+    def early(t, carry):
+        project_tile(t, 0, 4 * HEAD_DIM, lambda rows: jnp.zeros((TILE, WIDTH), F32), keep)
+        return carry
+
+    def late(t):
+        project_tile(t, 4 * HEAD_DIM, 2 * HEAD_DIM, lambda rows: acc[rows, :], finish)
+
+    lax.fori_loop(0, PARTS, early, 0)
     take_context(4)
+    risen(0, 0)
     take_context(5)
-    project(4 * HEAD_DIM, 2 * HEAD_DIM, lambda rows: acc[rows, :], finish)
 
     def part_rows(r):
         return pl.ds(r * TILE, TILE)
@@ -524,9 +531,15 @@
         (c_again if r in CACHE_PLUS else c_over)(r).wait_recv()
         go(c_far(r))
 
+    load_res.wait()
+    late(0)
     send_part(0)
+    late(1)
     send_part(1)
-    risen(0, 0)
+    late(2)
+    late(3)
+    save_hidden = pltpu.make_async_copy(hid.at[:, cols(x)], hidden_hbm, local_sem.at[2 * HEADS + 5])
+    save_hidden.start()
     risen(0, 1)
     sunk(4, 0, last=True)
     hand_on(0)
@@ -539,19 +552,32 @@
     for steps in range(-2, 6):
         for part in (0, 1):
             share(steps, part).wait_recv()
-    make_part(0)
-    hand_on(2)
-    make_part(1)
-    c_arrive(0)
-    hand_on(3)
-    make_part(2)
-    c_arrive(1)
-    complete(0)
-    make_part(3)
-    c_arrive(2)
-
     def head_cols(h):
         return pl.ds(pl.multiple_of(h * HEAD_DIM, HEAD_DIM), HEAD_DIM)
+
+    half = ROWS // 2
+
+    def c_own_first(h, carry):
+        g = h // 3
+        state = flash_step(
+            queries[:half, head_cols(h)],
+            cache[4, :half, head_cols(g)],
+            cache[4, :half, head_cols(g + 2)],
+            limits[0], None, "own",
+        )
+        put_state(refs, h, state, slice(0, half))
+        return carry
+
+    def c_own_last(h, carry):
+        g = h // 3
+        state = flash_step(
+            queries[half:, head_cols(h)],
+            cache[4, :, head_cols(g)],
+            cache[4, :, head_cols(g + 2)],
+            limits[0], None, "own", half,
+        )
+        put_state(refs, h, state, slice(half, ROWS))
+        return carry
 
     def step(h, slot, limit, state, past=None):
         g = h // 3
@@ -562,20 +588,35 @@
             limit, state, past,
         )
 
-    def c_own_keys(h, carry):
-        put_state(refs, h, step(h, 4, limits[0], None, "own"))
+    make_part(0)
+    hand_on(2)
+    make_part(1)
+    c_arrive(0)
+    lax.fori_loop(0, HEADS, c_own_first, 0)
+    hand_on(3)
+    make_part(2)
+    c_arrive(1)
+    complete(0)
+    make_part(3)
+    lax.fori_loop(0, HEADS, c_own_last, 0)
+    c_arrive(2)
+    c_forth(3).wait_recv()
+    go(c_near(3))
+
+    def line_keys(h, carry):
+        put_state(refs, h, step(h, 1, limits[2], get_state(refs, h)))
         return carry
 
-    lax.fori_loop(0, HEADS, c_own_keys, 0)
-    c_arrive(3)
+    lax.fori_loop(0, HEADS, line_keys, 0)
+    c_back(3).wait_recv()
+    go(c_over(3))
     complete(1)
     complete(2)
     for r in range(PARTS):
         c_near(r).wait_recv()
 
     def near_keys(h, carry):
-        state = step(h, 1, limits[2], get_state(refs, h))
-        put_state(refs, h, step(h, 2 * c, near_limit, state))
+        put_state(refs, h, step(h, 2 * c, near_limit, get_state(refs, h)))
         return carry
 
     lax.fori_loop(0, HEADS, near_keys, 0)
@@ -583,13 +624,22 @@
     for r in range(PARTS):
         c_far(r).wait_recv()
 
+    def save(h):
+        return pltpu.make_async_copy(
+            out_ref.at[:, head_cols(h)], out_hbm.at[:, head_cols(h)], local_sem.at[2 * HEADS + 6 + h]
+        )
+
     def far_keys(h, carry):
         state = step(h, 3, limits[4], get_state(refs, h))
         state = step(h, 2 * (1 - c), far_limit, state)
         out_ref[:, head_cols(h)] = (state[2] / state[1]).astype(BF16)
+        save(h).start()
         return carry
 
     lax.fori_loop(0, HEADS, far_keys, 0)
+    save_hidden.wait()
+    for h in range(HEADS):
+        save(h).wait()
     for copy in started:
         copy.wait_send()
     assert len(copies.made) == N_COPIES, len(copies.made)
@@ -598,16 +648,19 @@
 N_COPIES = 28 + 6 + 18 + 3 + 10 + 4 + 16 + 16 + 18
 
 
-def layer(doc, tail, q, res, gain, k, v, wo, wq, wc):
+def layer(doc, tail, gain, q, res, k, v, wo, wq, wc):
     any_spec = pl.BlockSpec(memory_space=pl.ANY)
     vmem = pl.BlockSpec(memory_space=pltpu.VMEM)
     smem = pl.BlockSpec(memory_space=pltpu.SMEM)
     return pl.pallas_call(
         layer_kernel,
         out_shape=(jax.ShapeDtypeStruct((ROWS, WIDTH), BF16),) * 2,
-        in_specs=[smem, smem, vmem, vmem, vmem] + [any_spec] * 5,
-        out_specs=(vmem, vmem),
+        in_specs=[smem, smem, vmem] + [any_spec] * 7,
+        out_specs=(any_spec, any_spec),
         scratch_shapes=[
+            pltpu.VMEM((ROWS, WIDTH), BF16),
+            pltpu.VMEM((ROWS, WIDTH), BF16),
+            pltpu.VMEM((ROWS, WIDTH), BF16),
             pltpu.VMEM((SLOTS, HEADS, 2, ROWS, HEAD_DIM), BF16),
             pltpu.VMEM((len(MINUS), 2, ROWS, HEAD_DIM), BF16),
             pltpu.VMEM((ROWS, D), BF16),
@@ -619,7 +672,7 @@
             pltpu.VMEM((SLOTS, ROWS, CACHE), BF16),
             pltpu.VMEM((len(CACHE_MINUS), TILE, CACHE), BF16),
             pltpu.VMEM((ROWS, WIDTH), BF16),
-            pltpu.SemaphoreType.DMA((2 * HEADS + 3,)),
+            pltpu.SemaphoreType.DMA((3 * HEADS + 6,)),
             pltpu.SemaphoreType.DMA((N_COPIES,)),
             pltpu.SemaphoreType.DMA((N_COPIES,)),
             pltpu.SemaphoreType.REGULAR,
@@ -628,15 +681,15 @@
             collective_id=0, has_side_effects=True, vmem_limit_bytes=60 * 1024 * 1024
         ),
         name="layer",
-    )(doc, tail, q, res, gain, k, v, wo, wq, wc)
+    )(doc, tail, gain, q, res, k, v, wo, wq, wc)
 
 
 def local(
     residual, q_self, k_self, v_self, w_out, norm_gain, w_query, w_cache, block_doc, tail_len
 ):
     return layer(
-        block_doc, tail_len, q_self, residual, norm_gain.reshape(1, D),
-        k_self, v_self, w_out, w_query, w_cache,
+        block_doc, tail_len, norm_gain.reshape(1, D), q_self, residual, k_self, v_self,
+        w_out, w_query, w_cache,
     )
 
 

time: 144 us -> 142 us (0.986); the launches traced: 143 us -> 142 us
  no operation moved by 1% of the time
where the time goes in v6:
time: 142 us
  Pallas kernels  137 us (96%)
  local copies, waits for them, and re-layouts  4.13 us (3%)
    pallas_call x1, Pallas kernels, layer(): pl.pallas_call(layer_kernel, out_shape=(jax.ShapeDtypeStruct((ROWS, WIDTH...  137 us
    unnamed x2, local copies, waits for them, and re-layouts  4.13 us

profile of v6, /device:TPU:9, one launch (start us, length us, event | category | flops | bytes accessed | tf_op | source)
XLA Modules:
  0.0 142.2 jit_solution(8621508884318328669)
XLA Ops:
  0.6 137.5 %layer.1 = (bf16[512,768]{1,0:T(8,128)(2,1)}, bf16[512,768]{1,0:T(8,128)(2,1)}) custom-call(s32[64]{0:T(128)} %doc_ref.1, s32[64]{0:T(128)} %tail_ref.1, f32[1,3072]{1,0:T(1,128)} %bitcast.1, bf16[512,768]{1,0:T(8,128)(2,1)} %q_hbm.1, bf16[512,768]{1,0:T(8,128)(2,1)} %res_hbm.1, bf16[512,768]{1,0:T(8,128)(2,1)} %k_hbm.1, bf16[512,768]{1,0:T(8,128)(2,1)} %v_hbm.1, ...), custom_call_target="tpu_custom_call" | custom-call | tf_op jit(solution)/shard_map/layer/pallas_call | solution.py:655
  138.1 2.1 %copy.14 = bf16[512,768]{1,0:T(8,128)(2,1)} copy(bf16[512,768]{1,0:T(8,128)(2,1)} %get-tuple-element.4) | data formatting | bytes 1572864
  140.2 2.1 %copy.15 = bf16[512,768]{1,0:T(8,128)(2,1)} copy(bf16[512,768]{1,0:T(8,128)(2,1)} %get-tuple-element.5) | data formatting | bytes 1572864
